TPU v7x, 32 devices: a whole 2x2x4 slice. The times are simulated.
32 devices in a mesh: dp: 8 (over z, y), section: 2 (over core), tensor: 2 (over x).
Axes of the slice: x: 2, y: 2, z: 4, core: 2. Of those that a mesh axis runs over, the one named last changes fastest.
Arguments:
- tower_input: bfloat16 [2, 1536, 1024], P('section', 'dp'), may hold values from -8 to 8
- up_weight: bfloat16 [2, 1024, 4096], P('section', None, 'tensor'), may hold values from -0.1875 to 0.1875
- down_weight: bfloat16 [2, 4096, 1024], P('section', 'tensor'), may hold values from -0.09375 to 0.09375
- pair: int32 [1536], P('dp'), may hold values from 0 to 1535, each once
- scale: float32 [1], replicated, may hold values from 4 to 16
- bias: float32 [1], replicated, may hold values from -4 to -1
Outputs:
- loss: float32 [1], replicated
- slide_grad: float32 [1536, 1024], P(('dp', 'section', 'tensor'))
- report_grad: float32 [1536, 1024], P(('dp', 'section', 'tensor'))
Inputs may be any that keep to these rules, and one draw needn't show every extreme that they name: `pair`: each report index appears exactly once.
All inputs are finite; a program needn't handle non-finite values.
Results may differ from a plain program's by a relative error of at most 0.00036.
Values may be sent and summed in bfloat16 or wider, within the bound.
A program may use at most 128 MiB of HBM per device.

v0:
```python
import functools
import math

import jax
import jax.numpy as jnp
from jax import lax
from jax.experimental import pallas as pl
from jax.experimental.pallas import tpu as pltpu
from jax.sharding import PartitionSpec as P

MESH = pl.DeviceIdType.MESH
INNER = 2
UP_PARTS = 4
DOWN_PARTS = 2
X, Y, ZM, ZP, CORE = range(5)
ROUTES = ("zxy", "zxy", "zyx", "yxz", "xzy", "zyx")
N_SUB = len(ROUTES)
ORDER = (
    (0, 0, 0, 0), (1, 0, 0, 0), (0, 0, 0, 1), (2, 0, 0, 0),
    (1, 0, 0, 1), (3, 0, 0, 0), (0, 0, 0, 2), (2, 0, 0, 1),
    (4, 0, 0, 0), (2, 0, 1, 0), (1, 0, 0, 2), (3, 0, 0, 1),
    (5, 0, 0, 0), (0, 1, 0, 0), (3, 0, 1, 0), (0, 0, 0, 3),
    (4, 0, 0, 1), (1, 1, 0, 0), (2, 0, 0, 2), (0, 1, 0, 1),
    (1, 0, 0, 3), (5, 0, 0, 1), (2, 0, 1, 1), (3, 0, 0, 2),
    (1, 1, 0, 1), (3, 0, 1, 1), (5, 0, 1, 0), (3, 1, 0, 0),
    (4, 0, 0, 2), (2, 0, 0, 3), (0, 1, 0, 2), (5, 0, 0, 2),
    (4, 1, 0, 0), (3, 0, 0, 3), (3, 0, 1, 2), (2, 0, 1, 2),
    (1, 1, 0, 2), (4, 0, 0, 3), (3, 1, 0, 1), (0, 1, 0, 3),
    (5, 0, 0, 3), (4, 1, 0, 1), (3, 1, 1, 0), (5, 0, 1, 1),
    (3, 1, 0, 2), (2, 0, 1, 3), (3, 0, 1, 3), (1, 1, 0, 3),
    (4, 1, 0, 2), (3, 1, 0, 3), (3, 1, 1, 1), (5, 0, 1, 2),
    (4, 1, 0, 3), (3, 1, 1, 2), (5, 0, 1, 3), (3, 1, 1, 3),
)


def wait_bytes(ref, sem):
    pltpu.make_async_copy(ref, ref, sem).wait()


def kernel(
    dims,
    scale_ref, bias_ref, pair_ref, x_ref, up_ref, down_ref,
    loss_out, mine_out, theirs_out,
    xs, up, down, hid, part, recv, emb, got, left, tile, tiles, scores, grad, loss_acc, loss_row, loss_all,
    x_sem, up_sem, down_sem, part_send, part_recv, own_send, near_send, fwd_send, got_recv,
    tile_send, tile_recv, grad_send, grad_recv, loss_send, loss_recv,
):
    n_dp, n_section, n_tensor, n_part, n_rows, width, total = dims
    n_outer = n_dp // INNER
    quarter = xs.shape[0] // (n_section * n_tensor)
    own_rows = n_section * quarter
    d, s, x = lax.axis_index("dp"), lax.axis_index("section"), lax.axis_index("tensor")
    z, y = d // INNER, lax.rem(d, INNER)
    ox, oy, os = 1 - x, 1 - y, 1 - s
    n_all = n_dp * n_section * n_tensor
    me = (d * n_section + s) * n_tensor + x

    def device(zz, yy, ss, xx):
        return {"dp": zz * INNER + yy, "section": ss, "tensor": xx}

    def device_of(n):
        return {
            "dp": n // (n_section * n_tensor),
            "section": lax.rem(n // n_tensor, n_section),
            "tensor": lax.rem(n, n_tensor),
        }

    n_sub_rows = own_rows // N_SUB

    def step_of(value, size, count):
        return sum((value >= i * size).astype(jnp.int32) for i in range(1, count))

    def make_ids():
        rows = n_section * n_tensor * quarter
        iota = lambda shape, dim: lax.broadcasted_iota(jnp.int32, shape, dim)
        pair = pair_ref[...].astype(jnp.float32)
        ids = (d * rows + iota((1, rows), 1)).astype(jnp.float32)
        first_core = jnp.broadcast_to(s, (1, rows)) == 0

        def natural(row, t):
            q = step_of(row, quarter, n_section)
            return (q * n_tensor + t) * quarter + (row - q * quarter)

        hit = iota((own_rows, rows), 1) == natural(iota((own_rows, rows), 0), x)
        kept = jnp.sum(jnp.where(hit, jnp.where(first_core, pair, ids), 0.0), axis=1, keepdims=True)
        left[...] = jnp.broadcast_to(kept, (own_rows, 128)).astype(jnp.int32)
        hit = iota((rows, rows), 0) == iota((rows, rows), 1)
        column = jnp.sum(jnp.where(hit, jnp.where(first_core, ids, pair), 0.0), axis=1, keepdims=True)
        lane = iota((rows, 128), 1)
        inner = step_of(lane, n_tensor * n_rows, INNER)
        lane = lane - inner * (n_tensor * n_rows)
        t = step_of(lane, n_rows, n_tensor)
        for c in range(n_part):
            hit = iota((rows, 128), 0) == natural(lane - t * n_rows + c * n_rows, t)
            line = jnp.sum(jnp.where(hit & (inner == y), column, 0.0), axis=0, keepdims=True)
            tile[c:c + 1] = line.astype(jnp.int32)
        tiles[d] = tile[...]

    x_copies = []
    for half, t in ((0, ox), (1, x)):
        for q in range(n_section):
            x_copies.append(pltpu.make_async_copy(
                x_ref.at[pl.ds(pl.multiple_of((q * n_tensor + t) * quarter, 16), quarter)],
                xs.at[pl.ds(half * own_rows + q * quarter, quarter)],
                x_sem.at[half * n_section + q],
            ))
    for c in x_copies:
        c.start()
    up_w = up.shape[1] // UP_PARTS
    down_w = down.shape[1] // DOWN_PARTS

    def up_copy(i):
        cols = pl.ds(pl.multiple_of(i * up_w, 128), up_w)
        return pltpu.make_async_copy(up_ref.at[:, cols], up.at[:, cols], up_sem.at[i])

    def down_copy(i):
        cols = pl.ds(pl.multiple_of(i * down_w, 128), down_w)
        return pltpu.make_async_copy(down_ref.at[:, cols], down.at[:, cols], down_sem.at[i])

    for i in range(UP_PARTS):
        up_copy(i).start()
    for i in range(DOWN_PARTS):
        down_copy(i).start()

    barrier = pltpu.get_barrier_semaphore()

    def greet(n, carry):
        @pl.when(n != me)
        def _():
            pl.semaphore_signal(barrier, inc=1, device_id=device_of(n), device_id_type=MESH)
        return carry

    lax.fori_loop(0, n_all, greet, 0)
    grad[...] = jnp.zeros_like(grad)
    loss_acc[...] = jnp.zeros_like(loss_acc)
    make_ids()
    for c in x_copies:
        c.wait()

    def first(half):
        rows = pl.ds(half * own_rows, own_rows)

        def body(i, carry):
            if half == 0:
                up_copy(i).wait()
            cols = pl.ds(pl.multiple_of(i * up_w, 128), up_w)
            h = jnp.dot(xs[rows], up[:, cols], preferred_element_type=jnp.float32)
            hid[rows, cols] = jax.nn.gelu(h).astype(jnp.bfloat16)
            return carry

        lax.fori_loop(0, UP_PARTS, body, 0)

    first(0)

    def second(i, carry):
        down_copy(i).wait()
        cols = pl.ds(pl.multiple_of(i * down_w, 128), down_w)
        part[0, :, cols] = jnp.dot(
            hid[0:own_rows], down[:, cols], preferred_element_type=jnp.float32
        )
        return carry

    lax.fori_loop(0, DOWN_PARTS, second, 0)
    pl.semaphore_wait(barrier, n_all - 1)

    def part_copy(c):
        rows = pl.ds(c * n_sub_rows, n_sub_rows)
        return pltpu.make_async_remote_copy(
            part.at[0, rows], recv.at[rows], part_send.at[c], part_recv.at[c],
            device_id=device(z, y, s, ox), device_id_type=MESH,
        )

    for c in range(N_SUB):
        part_copy(c).start()

    def tile_copy(n):
        return pltpu.make_async_remote_copy(
            tile, tiles.at[d], tile_send, tile_recv,
            device_id={"dp": n, "section": s, "tensor": x}, device_id_type=MESH,
        )

    def send_tile(n, carry):
        @pl.when(n != d)
        def _():
            tile_copy(n).start()
        return carry

    lax.fori_loop(0, n_dp, send_tile, 0)

    first(1)

    def second_own(i, carry):
        cols = pl.ds(pl.multiple_of(i * down_w, 128), down_w)
        part[1, :, cols] = jnp.dot(
            hid[own_rows:], down[:, cols], preferred_element_type=jnp.float32
        )
        return carry

    lax.fori_loop(0, DOWN_PARTS, second_own, 0)

    def slot(zz, yy, xx):
        return (zz * INNER + yy) * n_tensor + xx

    def place(c, sl):
        per = n_rows // n_sub_rows
        start = pl.multiple_of(sl * n_rows + c % per * n_sub_rows, n_sub_rows)
        return got.at[c // per, pl.ds(start, n_sub_rows)]

    def neighbour(way, ss):
        if way == X:
            return device(z, y, ss, ox)
        if way == Y:
            return device(z, oy, ss, x)
        if way == ZM:
            return device(z - 1, y, ss, x)
        if way == ZP:
            return device(z + 1, y, ss, x)
        return device(z, y, ss, x)

    def own_copy(c, way):
        sl = slot(z, y, x)
        return pltpu.make_async_remote_copy(
            emb.at[pl.ds(c * n_sub_rows, n_sub_rows)], place(c, sl), own_send.at[c, way],
            got_recv.at[c, sl], device_id=neighbour(way, os), device_id_type=MESH,
        )

    def fwd_copy(c, sl, way, sem):
        return pltpu.make_async_remote_copy(
            place(c, sl), place(c, sl), sem, got_recv.at[c, sl],
            device_id=neighbour(way, s), device_id_type=MESH,
        )

    def guarded(way, act):
        if way == ZM:
            pl.when(z > 0)(act)
        elif way == ZP:
            pl.when(z < n_outer - 1)(act)
        else:
            act()

    def own_all(c, begin):
        for way in (ZM, ZP, Y, X, CORE):
            guarded(way, lambda: own_copy(c, way).start() if begin else own_copy(c, way).wait_send())

    def ways(c, rx, ry, far, side):
        moved = {"x": rx, "y": ry, "z": far}
        route = ROUTES[c]
        done = max((i + 1 for i in range(3) if moved[route[i]]), default=0)
        if not done:
            return ()
        out = {"x": (X,), "y": (Y,), "z": (ZM, ZP)}
        onward = (ZM if side > 0 else ZP,) if route[done - 1] == "z" else ()
        return sum((out[i] for i in route[done:]), onward)

    def handle(c, rx, ry, begin, k=0, side=0):
        far = side != 0
        sz = z + side * k
        sl = slot(sz, oy if ry else y, ox if rx else x)

        def act():
            if begin:
                wait_bytes(place(c, sl), got_recv.at[c, sl])
            for way in ways(c, rx, ry, far, side):
                if way == ZP and not far:
                    sem = near_send.at[c, rx * INNER + ry]
                else:
                    sem = fwd_send.at[c, sl, min(way, ZM)]
                copy = fwd_copy(c, sl, way, sem)
                guarded(way, copy.start if begin else copy.wait_send)

        if far:
            pl.when((sz >= 0) & (sz < n_outer))(act)
        else:
            act()

    def far_loop(begin, blocks):
        def body(k, carry):
            for c, rx, ry in blocks:
                for side in (-1, 1):
                    handle(c, rx, ry, begin, k, side)
            return carry
        lax.fori_loop(1, n_outer, body, 0)

    def produce(c):
        rows = pl.ds(c * n_sub_rows, n_sub_rows)
        part_copy(c).wait_recv()
        raw = (part[1, rows] + recv[rows]) + xs[
            pl.ds(own_rows + c * n_sub_rows, n_sub_rows)
        ].astype(jnp.float32)
        norms = lax.rsqrt(jnp.sum(raw * raw, axis=-1, keepdims=True) + 1e-06)
        emb[rows] = (raw * norms).astype(jnp.bfloat16)
        own_all(c, True)

    scale_value, bias_value = scale_ref[0], bias_ref[0]
    batch = math.gcd(4, n_outer)
    group = batch * INNER * n_tensor * n_rows
    group_lanes = lambda g: pl.ds(pl.multiple_of(g * group, 128), group)

    def score(c):
        def body(g, carry):
            block = got[c, pl.ds(pl.multiple_of(g * group, group), group)]
            logits = scale_value * lax.dot_general(
                emb[...], block, (((1,), (1,)), ((), ())), preferred_element_type=jnp.float32
            ) + bias_value
            lines = []
            for j in range(batch):
                at = (g * batch + j) * INNER
                lines.append(sum(tiles[at + i, c:c + 1] for i in range(INNER)))
            for j in range(batch):
                sign = jnp.where(left[...] == lines[j], 1.0, -1.0).astype(jnp.float32)
                u = -sign * logits[:, j * 128:(j + 1) * 128]
                e = jnp.exp(-jnp.abs(u))
                loss_acc[...] += jnp.maximum(u, 0.0) + jnp.log1p(e)
                sigmoid = jnp.where(u >= 0, 1.0, e) / (1.0 + e)
                lanes = pl.ds(pl.multiple_of(g * group + j * 128, 128), 128)
                scores[:, lanes] = (-scale_value * sign * sigmoid).astype(jnp.bfloat16)
            return carry

        lax.fori_loop(0, n_outer // batch, body, 0)

    def collect(c):
        def body(g, carry):
            block = got[c, pl.ds(pl.multiple_of(g * group, group), group)]
            grad[...] += jnp.dot(
                scores[:, group_lanes(g)], block, preferred_element_type=jnp.float32
            )
            return carry

        lax.fori_loop(0, n_outer // batch, body, 0)

    shifts = [(c, rx, ry) for c in range(N_SUB) for rx in (0, 1) for ry in (0, 1)]
    passed = [b for b in sorted(shifts, key=lambda b: b[1] + b[2]) if ways(*b, True, 1)]
    table_k = max(k for _, _, _, k in ORDER)

    def pass_on(begin):
        for c, rx, ry, k in ORDER:
            if k >= n_outer:
                continue
            if k:
                for side in (-1, 1):
                    handle(c, rx, ry, begin, k, side)
            elif rx or ry:
                handle(c, rx, ry, begin)
            elif begin:
                produce(c)
            else:
                own_all(c, False)

        def body(k, carry):
            for c, rx, ry in passed:
                for side in (-1, 1):
                    handle(c, rx, ry, begin, k, side)
            return carry

        if table_k + 1 < n_outer:
            lax.fori_loop(table_k + 1, n_outer, body, 0)

    def finish(c):
        per = n_rows // n_sub_rows
        blocks = [b for b in shifts if b[0] // per == c]
        for b in blocks:
            if b[1:] == (0, 0) or not ways(*b, False, 0):
                handle(*b, True)
        ends = [b for b in blocks if not ways(*b, True, 1)]

        def body(k, carry):
            for b in ends:
                for side in (-1, 1):
                    handle(*b, True, k, side)
            return carry

        lax.fori_loop(1, n_outer, body, 0)

    pass_on(True)
    wait_bytes(tiles.at[pl.ds(0, n_dp - 1)], tile_recv)

    def loss_copy(n):
        return pltpu.make_async_remote_copy(
            loss_row, loss_all.at[slot(z, y, x)], loss_send, loss_recv,
            device_id=device_of(n), device_id_type=MESH,
        )

    def send_loss(n, carry):
        loss_copy(lax.rem(me + n, n_all)).start()
        return carry

    for c in range(n_part):
        finish(c)
        score(c)
        if c == n_part - 1:
            loss_row[...] = jnp.sum(loss_acc[...], axis=0, keepdims=True)

            @pl.when(s == 0)
            def _():
                loss_all[slot(z, y, x)] = loss_row[...]
                lax.fori_loop(1, n_all, send_loss, 0)

        collect(c)

    grad_copy = pltpu.make_async_remote_copy(
        grad.at[pl.ds(pl.multiple_of(os * quarter, 16), quarter)], theirs_out, grad_send, grad_recv,
        device_id=device(z, y, os, x), device_id_type=MESH,
    )
    grad_copy.start()
    mine_out[...] = grad[pl.ds(pl.multiple_of(s * quarter, 16), quarter)]
    for c in range(N_SUB):
        part_copy(c).wait_send()
    wait_bytes(tiles.at[pl.ds(0, n_dp - 1)], tile_send)
    pass_on(False)
    grad_copy.wait()
    n_chips = n_dp * n_tensor

    @pl.when(s == 0)
    def _():
        wait_bytes(loss_all.at[pl.ds(0, n_all - 1)], loss_send)
        wait_bytes(loss_all.at[pl.ds(0, n_chips - 1)], loss_recv)

    @pl.when(s != 0)
    def _():
        wait_bytes(loss_all.at[pl.ds(0, n_chips)], loss_recv)

    loss_out[0] = jnp.sum(loss_all[0:n_chips]) / total


def local(tower_input, up_weight, down_weight, pair, scale, bias):
    n_dp = lax.axis_size("dp")
    n_section = lax.axis_size("section")
    n_tensor = lax.axis_size("tensor")
    inputs, up_w, down_w = tower_input[0], up_weight[0], down_weight[0]
    rows, width = inputs.shape
    hidden = up_w.shape[1]
    group = n_section * n_tensor
    quarter = rows // group
    own_rows = n_section * quarter
    total = n_dp * rows
    n_rows = 128 // (INNER * n_tensor)
    n_part = own_rows // n_rows
    chips = n_dp * n_tensor

    f32, bf16 = jnp.float32, jnp.bfloat16
    vmem = pl.BlockSpec(memory_space=pltpu.VMEM)
    smem = pl.BlockSpec(memory_space=pltpu.SMEM)
    hbm = pl.BlockSpec(memory_space=pl.ANY)
    dma = pltpu.SemaphoreType.DMA
    n_all = n_dp * group
    dims = (n_dp, n_section, n_tensor, n_part, n_rows, width, total)
    loss, mine, theirs = pl.pallas_call(
        functools.partial(kernel, dims),
        out_shape=(
            jax.ShapeDtypeStruct((1,), f32),
            jax.ShapeDtypeStruct((quarter, width), f32),
            jax.ShapeDtypeStruct((quarter, width), f32),
        ),
        in_specs=[smem, smem, vmem, hbm, hbm, hbm],
        out_specs=(smem, vmem, vmem),
        scratch_shapes=[
            pltpu.VMEM((rows, width), bf16),
            pltpu.VMEM((width, hidden), bf16),
            pltpu.VMEM((hidden, width), bf16),
            pltpu.VMEM((rows, hidden), bf16),
            pltpu.VMEM((2, own_rows, width), f32),
            pltpu.VMEM((own_rows, width), f32),
            pltpu.VMEM((own_rows, width), bf16),
            pltpu.VMEM((n_part, chips * n_rows, width), bf16),
            pltpu.VMEM((own_rows, 128), jnp.int32),
            pltpu.VMEM((8, 128), jnp.int32),
            pltpu.VMEM((n_dp, 8, 128), jnp.int32),
            pltpu.VMEM((own_rows, chips * n_rows), bf16),
            pltpu.VMEM((own_rows, width), f32),
            pltpu.VMEM((own_rows, 128), f32),
            pltpu.VMEM((1, 128), f32),
            pltpu.VMEM((n_all, 1, 128), f32),
            dma((group,)),
            dma((UP_PARTS,)),
            dma((DOWN_PARTS,)),
            dma((N_SUB,)),
            dma((N_SUB,)),
            dma((N_SUB, 5)),
            dma((N_SUB, n_tensor * INNER)),
            dma((N_SUB, chips, 3)),
            dma((N_SUB, chips)),
            dma, dma, dma, dma, dma, dma,
        ],
        compiler_params=pltpu.CompilerParams(
            collective_id=0, has_side_effects=True, vmem_limit_bytes=60 * 1024 * 1024
        ),
    )(scale, bias, pair.reshape(1, rows), inputs, up_w, down_w)
    first_core = lax.axis_index("section") == 0
    return (
        loss,
        jnp.where(first_core, mine, theirs),
        jnp.where(first_core, theirs, mine),
    )


def solution(mesh):
    return jax.shard_map(
        local,
        mesh=mesh,
        in_specs=(
            P("section", "dp", None),
            P("section", None, "tensor"),
            P("section", "tensor", None),
            P("dp"),
            P(),
            P(),
        ),
        out_specs=(P(), P(("dp", "section", "tensor"), None), P(("dp", "section", "tensor"), None)),
        check_vma=False,
    )
```

profile of v0, /device:TPU:1, one launch (start us, length us, event | category | flops | bytes accessed | tf_op | source)
XLA Modules:
  0.0 58.0 jit_solution(5326817607732398827)
XLA Ops:
  1.9 52.4 %shard_map.85 = (f32[1]{0:T(128)}, f32[48,1024]{1,0:T(8,128)}, f32[48,1024]{1,0:T(8,128)}) custom-call(f32[1]{0:T(128)S(6)} %copy.10.scale_ref, f32[1]{0:T(128)S(6)} %copy.11.bias_ref, s32[1,192]{1,0:T(1,128)} %bitcast.7, bf16[192,1024]{1,0:T(8,128)(2,1)} %bitcast.6, bf16[1024,2048]{1,0:T(8,128)(2,1)} %bitcast.4, bf16[2048,1024]{1,0:T(8,128)(2,1)} %bitcast.5), custom_call_target="tpu_custom_call" | custom-call | tf_op jit(solution)/shard_map/pallas_call | solution.py:447
  54.3 1.8 %broadcast_select_fusion = (f32[48,1024]{1,0:T(8,128)}, f32[48,1024]{1,0:T(8,128)}) fusion(f32[48,1024]{1,0:T(8,128)} %get-tuple-element.8, f32[48,1024]{1,0:T(8,128)} %get-tuple-element.7, pred[]{:T(512)S(6)} %eq.3), kind=kLoop, calls=%fused_computation | loop fusion | flops 98304 | bytes 786433 | tf_op jit(solution)/shard_map/jit(_where)/select_n | solution.py:492
where the time goes:
time: 58.8 us; the launch traced here: 58 us
  Pallas kernels  52.4 us (89%)
  between operations  3.76 us (6%)
  other arithmetic  1.8 us (3%)
    pallas_call x1, Pallas kernels, local(): pl.pallas_call(functools.partial(kernel, dims), out_shape=(jax.ShapeDtype...  52.4 us
    select_n x1, other arithmetic, local(): jnp.where(first_core, theirs, mine)  1.8 us

commit v1 on v0

v1 whole, which is shorter than its diff:
```python
import functools

import jax
import jax.numpy as jnp
from jax import lax
from jax.experimental import pallas as pl
from jax.experimental.pallas import tpu as pltpu
from jax.sharding import PartitionSpec as P

MESH = pl.DeviceIdType.MESH
INNER = 2
PAIR = 2
UP_PARTS = 4
DOWN_PARTS = 2
N_SUB = 6
TOP = 32767.0


def events():
    hop = {"P": 0.0, "A": 2.3, "B": 2.9, "D": 5.2}
    found = [(c * 0.8 + at, "PABD".index(kind), kind, c) for kind, at in hop.items() for c in range(N_SUB)]
    return [(kind, c) for _, _, kind, c in sorted(found)]


def wait_bytes(ref, sem):
    pltpu.make_async_copy(ref, ref, sem).wait()


def iota(shape, dim):
    return lax.broadcasted_iota(jnp.int32, shape, dim)


def step_of(value, size, count):
    return sum((value >= i * size).astype(jnp.int32) for i in range(1, count))


def to_row(column, lanes=128):
    rows = column.shape[0]
    hit = iota((rows, lanes), 0) == iota((rows, lanes), 1)
    return jnp.sum(jnp.where(hit, column, 0.0), axis=0, keepdims=True)


def to_column(row, rows):
    hit = iota((rows, row.shape[1]), 0) == iota((rows, row.shape[1]), 1)
    return jnp.sum(jnp.where(hit, row, 0.0), axis=1, keepdims=True)


def to_fixed(value):
    top = jnp.maximum(jnp.max(jnp.abs(value), axis=-1, keepdims=True), 1e-30)
    fixed = jnp.round(value * (TOP / top)).astype(jnp.int32).astype(jnp.int16)
    return fixed, top * (1.0 / TOP)


def from_fixed(fixed, unit):
    return fixed.astype(jnp.int32).astype(jnp.float32) * unit


def kernel(
    dims,
    scale_ref, bias_ref, pair_ref, x_ref, up_ref, down_ref,
    loss_out, slide_out, report_out,
    xs, up, down, hid, part, fixed, fixed_in, unit, unit_in, units, pairs, left, right,
    held, other, scores, grad, sent, sent_unit, got, got_unit, twin, loss_acc, loss_row, loss_all,
    x_sem, up_sem, down_sem, part_send, part_recv, unit_send, unit_recv, pair_send, pair_recv,
    held_recv, near_send, far_send, fwd_send, core_send, other_recv,
    sent_send, sent_unit_send, got_recv, got_unit_recv, twin_send, twin_recv, loss_send, loss_recv,
):
    n_dp, n_section, n_tensor, n_half, total = dims
    quarter = xs.shape[0] // (n_section * n_tensor)
    own_rows = n_section * quarter
    rows_dp = xs.shape[0]
    d, s, x = lax.axis_index("dp"), lax.axis_index("section"), lax.axis_index("tensor")
    y, low, half = lax.rem(d, INNER), lax.rem(d // INNER, PAIR), d // (INNER * PAIR)
    n_all = n_dp * n_section * n_tensor
    me = (d * n_section + s) * n_tensor + x
    tile_blocks = 2 * PAIR
    tile_rows = tile_blocks * own_rows
    n_tiles = n_half // PAIR

    def device_of(n):
        return {
            "dp": n // (n_section * n_tensor),
            "section": lax.rem(n // n_tensor, n_section),
            "tensor": lax.rem(n, n_tensor),
        }

    def pick(t, first, second):
        return first + t * (second - first)

    def member(t, a, b, core):
        at_y, at_low, at_half = pick(t, y, a), pick(t, b, low), pick(t, half, b)
        return {
            "dp": (at_half * PAIR + at_low) * INNER + at_y, "section": core, "tensor": pick(t, a, x)
        }

    def place_of(t):
        return pick(t, x, y), pick(t, low, half), pick(t, PAIR, n_half)

    my_a, my_b, my_n = place_of(s)
    mine = my_b * 2 + my_a
    partner = {"dp": d, "section": 1 - s, "tensor": x}

    def others(count, act):
        if n_half == PAIR:
            act(1)
        else:
            def body(k, carry):
                act(k)
                return carry
            lax.fori_loop(1, count, body, 0)

    x_copies = []
    for side, t in ((0, 1 - x), (1, x)):
        for q in range(n_section):
            x_copies.append(pltpu.make_async_copy(
                x_ref.at[pl.ds(pl.multiple_of((q * n_tensor + t) * quarter, 16), quarter)],
                xs.at[pl.ds(side * own_rows + q * quarter, quarter)],
                x_sem.at[side * n_section + q],
            ))
    for c in x_copies:
        c.start()
    up_w = up.shape[1] // UP_PARTS
    down_w = down.shape[1] // DOWN_PARTS

    def up_copy(i):
        cols = pl.ds(pl.multiple_of(i * up_w, 128), up_w)
        return pltpu.make_async_copy(up_ref.at[:, cols], up.at[:, cols], up_sem.at[i])

    def down_copy(i):
        cols = pl.ds(pl.multiple_of(i * down_w, 128), down_w)
        return pltpu.make_async_copy(down_ref.at[:, cols], down.at[:, cols], down_sem.at[i])

    for i in range(UP_PARTS):
        up_copy(i).start()
    for i in range(DOWN_PARTS):
        down_copy(i).start()

    barrier = pltpu.get_barrier_semaphore()

    def greet(n, carry):
        @pl.when(n != me)
        def _():
            pl.semaphore_signal(barrier, inc=1, device_id=device_of(n), device_id_type=MESH)
        return carry

    lax.fori_loop(0, n_all, greet, 0)
    loss_acc[...] = jnp.zeros_like(loss_acc)

    def natural(lane, t):
        q = step_of(lane, quarter, n_section)
        return (q * n_tensor + t) * quarter + (lane - q * quarter)

    def order_pairs():
        column = to_column(pair_ref[...].astype(jnp.float32), rows_dp)
        lane = iota((rows_dp, rows_dp), 1)
        t = step_of(lane, own_rows, n_tensor)
        hit = iota((rows_dp, rows_dp), 0) == natural(lane - t * own_rows, t)
        pairs[low] = jnp.sum(jnp.where(hit, column, 0.0), axis=0, keepdims=True).astype(jnp.int32)

    order_pairs()

    def report_ids(index):
        block = step_of(index, own_rows, tile_blocks)
        b = step_of(block, 2, PAIR)
        home = (b * PAIR + low) * INNER + (block - 2 * b)
        return home * rows_dp + natural(index - block * own_rows, x)

    for c in x_copies:
        c.wait()

    def first(side):
        rows = pl.ds(side * own_rows, own_rows)

        def body(i, carry):
            if side == 0:
                up_copy(i).wait()
            cols = pl.ds(pl.multiple_of(i * up_w, 128), up_w)
            h = jnp.dot(xs[rows], up[:, cols], preferred_element_type=jnp.float32)
            hid[rows, cols] = jax.nn.gelu(h).astype(jnp.bfloat16)
            return carry

        lax.fori_loop(0, UP_PARTS, body, 0)

    def second(side):
        def body(i, carry):
            if side == 0:
                down_copy(i).wait()
            cols = pl.ds(pl.multiple_of(i * down_w, 128), down_w)
            part[:, cols] = jnp.dot(
                hid[side * own_rows:(side + 1) * own_rows], down[:, cols],
                preferred_element_type=jnp.float32,
            )
            return carry

        lax.fori_loop(0, DOWN_PARTS, body, 0)

    first(0)
    second(0)
    values, units_of = to_fixed(part[...])
    fixed[...] = values
    unit[...] = to_row(units_of)
    pl.semaphore_wait(barrier, n_all - 1)

    sub = own_rows // N_SUB
    across = {"dp": d, "section": s, "tensor": 1 - x}

    def part_copy(c):
        rows = pl.ds(c * sub, sub)
        return pltpu.make_async_remote_copy(
            fixed.at[rows], fixed_in.at[rows], part_send.at[c], part_recv.at[c],
            device_id=across, device_id_type=MESH,
        )

    unit_copy = pltpu.make_async_remote_copy(
        unit, unit_in, unit_send, unit_recv, device_id=across, device_id_type=MESH
    )
    unit_copy.start()
    for c in range(N_SUB):
        part_copy(c).start()
    pair_copy = pltpu.make_async_remote_copy(
        pairs.at[low], pairs.at[low], pair_send, pair_recv,
        device_id={"dp": (half * PAIR + 1 - low) * INNER + y, "section": s, "tensor": x},
        device_id_type=MESH,
    )
    pair_copy.start()

    first(1)
    second(1)
    pair_copy.wait_recv()

    @pl.when(s == 0)
    def _():
        for b in range(PAIR):
            column = to_column(pairs[b].astype(jnp.float32), rows_dp).astype(jnp.int32)
            left[b * rows_dp:(b + 1) * rows_dp] = jnp.broadcast_to(column, (rows_dp, 128))
        right[...] = report_ids(iota((1, tile_rows), 1))

    @pl.when(s != 0)
    def _():
        left[...] = report_ids(iota((tile_rows, 128), 0))
        for b in range(PAIR):
            right[:, b * rows_dp:(b + 1) * rows_dp] = pairs[b]

    unit_copy.wait_recv()
    units[...] = jnp.broadcast_to(to_column(unit_in[...], own_rows), (own_rows, 128))

    def piece(block, c):
        return held.at[block, pl.ds(c * sub, sub)]

    def held_copy(block, c, to, sem):
        return pltpu.make_async_remote_copy(
            piece(block, c), piece(block, c), sem, held_recv.at[c, block],
            device_id=to, device_id_type=MESH,
        )

    def core_copy(block, c):
        return pltpu.make_async_remote_copy(
            piece(block, c), other.at[block, pl.ds(c * sub, sub)], core_send.at[c, block],
            other_recv.at[block], device_id=partner, device_id_type=MESH,
        )

    beside = member(s, 1 - my_a, my_b, s)

    def at_b(k):
        return lax.rem(my_b + k, my_n)

    def beyond(k):
        return member(s, my_a, at_b(k), s)

    def arrived(block, c, begin):
        if begin:
            wait_bytes(piece(block, c), held_recv.at[c, block])
            core_copy(block, c).start()
        else:
            core_copy(block, c).wait_send()

    def act_on(kind, c, begin):
        run = lambda copy: copy.start() if begin else copy.wait_send()
        if kind == "P":
            if begin:
                rows = pl.ds(c * sub, sub)
                part_copy(c).wait_recv()
                theirs = from_fixed(fixed_in[rows], units[rows, 0:1])
                raw = (part[rows] + theirs) + xs[
                    pl.ds(own_rows + c * sub, sub)
                ].astype(jnp.float32)
                norms = lax.rsqrt(jnp.sum(raw * raw, axis=-1, keepdims=True) + 1e-06)
                held[mine, rows] = (raw * norms).astype(jnp.bfloat16)
            run(held_copy(mine, c, beside, near_send.at[c]))
            others(my_n, lambda k: run(held_copy(mine, c, beyond(k), far_send.at[c, k])))
            run(core_copy(mine, c))
        elif kind == "A":
            block = my_b * 2 + 1 - my_a
            arrived(block, c, begin)

            @pl.when(s == 0)
            def _():
                others(my_n, lambda k: run(held_copy(block, c, beyond(k), fwd_send.at[c, k])))
        elif kind == "B":
            def from_b(k):
                block = at_b(k) * 2 + my_a
                arrived(block, c, begin)

                @pl.when(s != 0)
                def _():
                    run(held_copy(block, c, beside, fwd_send.at[c, k]))

            others(my_n, from_b)
        else:
            others(my_n, lambda k: arrived(at_b(k) * 2 + 1 - my_a, c, begin))

    for kind, c in events():
        act_on(kind, c, True)

    def other_block(block, carry):
        wait_bytes(other.at[block], other_recv.at[block])
        return carry

    if n_half == PAIR:
        for block in range(tile_blocks):
            other_block(block, 0)
    else:
        lax.fori_loop(0, 2 * pick(s, n_half, PAIR), other_block, 0)

    scale_value, bias_value = scale_ref[0], bias_ref[0]
    width = held.shape[2]

    def score(tile):
        m_tile, t_tile = pick(s, 0, tile), pick(s, tile, 0)
        rows = held[pl.ds(m_tile * tile_blocks, tile_blocks)].reshape(tile_rows, width)
        columns = other[pl.ds(t_tile * tile_blocks, tile_blocks)].reshape(tile_rows, width)
        logits = scale_value * lax.dot_general(
            rows, columns, (((1,), (1,)), ((), ())), preferred_element_type=jnp.float32
        ) + bias_value
        shift = (1 - 2 * s) * tile * (PAIR * PAIR * INNER * rows_dp)
        for j in range(tile_rows // 128):
            lanes = slice(j * 128, (j + 1) * 128)
            sign = jnp.where(left[...] == right[:, lanes] + shift, 1.0, -1.0).astype(jnp.float32)
            u = -sign * logits[:, lanes]
            e = jnp.exp(-jnp.abs(u))
            loss_acc[...] += jnp.maximum(u, 0.0) + jnp.log1p(e)
            sigmoid = jnp.where(u >= 0, 1.0, e) / (1.0 + e)
            scores[:, lanes] = (-scale_value * sign * sigmoid).astype(jnp.bfloat16)
        return m_tile, columns

    if n_tiles > 1:
        def clear(block, carry):
            grad[block] = jnp.zeros_like(grad[block])
            return carry

        lax.fori_loop(0, 2 * my_n, clear, 0)

        def tile_step(tile, carry):
            m_tile, columns = score(tile)
            for k in range(tile_blocks):
                grad[m_tile * tile_blocks + k] += jnp.dot(
                    scores[k * own_rows:(k + 1) * own_rows], columns,
                    preferred_element_type=jnp.float32,
                )
            return carry

        lax.fori_loop(0, n_tiles, tile_step, 0)
    else:
        _, columns = score(0)

    slot = d * n_tensor + x

    def loss_copy(n):
        return pltpu.make_async_remote_copy(
            loss_row, loss_all.at[slot], loss_send, loss_recv,
            device_id=device_of(n), device_id_type=MESH,
        )

    def send_loss(n, carry):
        loss_copy(lax.rem(me + n, n_all)).start()
        return carry

    def sent_copy(block, a, b, h):
        return pltpu.make_async_remote_copy(
            sent.at[block, pl.ds(h * quarter, quarter)], got.at[s, mine], sent_send.at[block, h],
            got_recv.at[s, mine], device_id=member(s, a, b, h), device_id_type=MESH,
        )

    def sent_unit_copy(block, a, b, h):
        return pltpu.make_async_remote_copy(
            sent_unit.at[block, h], got_unit.at[s, mine], sent_unit_send.at[block, h],
            got_unit_recv.at[s, mine], device_id=member(s, a, b, h), device_id_type=MESH,
        )

    def finish_block(block):
        if n_tiles == 1:
            grad[block] = jnp.dot(
                scores[pl.ds(pl.multiple_of(block * own_rows, 16), own_rows)], columns,
                preferred_element_type=jnp.float32,
            )

    def send_block(a, k, begin):
        b = at_b(k)
        block = b * 2 + a
        if begin:
            finish_block(block)
            values, units_of = to_fixed(grad[block])
            sent[block] = values
            for h in range(n_section):
                sent_unit[block, h] = to_row(units_of[h * quarter:(h + 1) * quarter])
        for h in range(n_section):
            for copy in (sent_unit_copy(block, a, b, h), sent_copy(block, a, b, h)):
                copy.start() if begin else copy.wait_send()

    def send_all(begin):
        others(my_n, lambda k: send_block(1 - my_a, k, begin))
        others(my_n, lambda k: send_block(my_a, k, begin))
        send_block(1 - my_a, 0, begin)

    send_all(True)
    finish_block(mine)
    twin_copy = pltpu.make_async_remote_copy(
        grad.at[mine, pl.ds(pl.multiple_of((1 - s) * quarter, 16), quarter)], twin,
        twin_send, twin_recv, device_id=partner, device_id_type=MESH,
    )
    twin_copy.start()
    loss_row[...] = jnp.sum(loss_acc[...], axis=0, keepdims=True)

    @pl.when(s == 0)
    def _():
        loss_all[slot] = loss_row[...]
        lax.fori_loop(1, n_all, send_loss, 0)

    def add_got(t, a, b, out):
        block = b * 2 + a
        wait_bytes(got_unit.at[t, block], got_unit_recv.at[t, block])
        wait_bytes(got.at[t, block], got_recv.at[t, block])
        out[...] += from_fixed(got[t, block], to_column(got_unit[t, block], quarter))

    def collect(t, out):
        a, b, count = place_of(t)
        add_got(t, 1 - a, b, out)
        others(count, lambda k: add_got(t, a, lax.rem(b + k, count), out))
        others(count, lambda k: add_got(t, 1 - a, lax.rem(b + k, count), out))

    own_sum = grad[mine, pl.ds(pl.multiple_of(s * quarter, 16), quarter)]
    twin_copy.wait_recv()

    @pl.when(s == 0)
    def _():
        slide_out[...] = own_sum
        report_out[...] = twin[...]

    @pl.when(s != 0)
    def _():
        report_out[...] = own_sum
        slide_out[...] = twin[...]

    collect(0, slide_out)
    collect(1, report_out)

    for c in range(N_SUB):
        part_copy(c).wait_send()
    unit_copy.wait_send()
    pair_copy.wait_send()
    for kind, c in events():
        act_on(kind, c, False)
    send_all(False)
    twin_copy.wait_send()
    n_chips = n_dp * n_tensor

    @pl.when(s == 0)
    def _():
        wait_bytes(loss_all.at[pl.ds(0, n_all - 1)], loss_send)
        wait_bytes(loss_all.at[pl.ds(0, n_chips - 1)], loss_recv)

    @pl.when(s != 0)
    def _():
        wait_bytes(loss_all.at[pl.ds(0, n_chips)], loss_recv)

    loss_out[0] = jnp.sum(loss_all[0:n_chips]) / total


def local(tower_input, up_weight, down_weight, pair, scale, bias):
    n_dp = lax.axis_size("dp")
    n_section = lax.axis_size("section")
    n_tensor = lax.axis_size("tensor")
    inputs, up_w, down_w = tower_input[0], up_weight[0], down_weight[0]
    rows, width = inputs.shape
    hidden = up_w.shape[1]
    group = n_section * n_tensor
    quarter = rows // group
    own_rows = n_section * quarter
    total = n_dp * rows
    n_half = n_dp // (INNER * PAIR)
    blocks = 2 * n_half
    tile_rows = 2 * PAIR * own_rows

    f32, bf16, i16, i32 = jnp.float32, jnp.bfloat16, jnp.int16, jnp.int32
    vmem = pl.BlockSpec(memory_space=pltpu.VMEM)
    smem = pl.BlockSpec(memory_space=pltpu.SMEM)
    hbm = pl.BlockSpec(memory_space=pl.ANY)
    dma = pltpu.SemaphoreType.DMA
    n_all = n_dp * group
    dims = (n_dp, n_section, n_tensor, n_half, total)
    return pl.pallas_call(
        functools.partial(kernel, dims),
        out_shape=(
            jax.ShapeDtypeStruct((1,), f32),
            jax.ShapeDtypeStruct((quarter, width), f32),
            jax.ShapeDtypeStruct((quarter, width), f32),
        ),
        in_specs=[smem, smem, vmem, hbm, hbm, hbm],
        out_specs=(smem, vmem, vmem),
        scratch_shapes=[
            pltpu.VMEM((rows, width), bf16),
            pltpu.VMEM((width, hidden), bf16),
            pltpu.VMEM((hidden, width), bf16),
            pltpu.VMEM((rows, hidden), bf16),
            pltpu.VMEM((own_rows, width), f32),
            pltpu.VMEM((own_rows, width), i16),
            pltpu.VMEM((own_rows, width), i16),
            pltpu.VMEM((1, 128), f32),
            pltpu.VMEM((1, 128), f32),
            pltpu.VMEM((own_rows, 128), f32),
            pltpu.VMEM((PAIR, 1, rows), i32),
            pltpu.VMEM((tile_rows, 128), i32),
            pltpu.VMEM((1, tile_rows), i32),
            pltpu.VMEM((blocks, own_rows, width), bf16),
            pltpu.VMEM((blocks, own_rows, width), bf16),
            pltpu.VMEM((tile_rows, tile_rows), bf16),
            pltpu.VMEM((blocks, own_rows, width), f32),
            pltpu.VMEM((blocks, own_rows, width), i16),
            pltpu.VMEM((blocks, n_section, 1, 128), f32),
            pltpu.VMEM((n_section, blocks, quarter, width), i16),
            pltpu.VMEM((n_section, blocks, 1, 128), f32),
            pltpu.VMEM((quarter, width), f32),
            pltpu.VMEM((tile_rows, 128), f32),
            pltpu.VMEM((1, 128), f32),
            pltpu.VMEM((n_all, 1, 128), f32),
            dma((group,)),
            dma((UP_PARTS,)),
            dma((DOWN_PARTS,)),
            dma((N_SUB,)),
            dma((N_SUB,)),
            dma, dma, dma, dma,
            dma((N_SUB, blocks)),
            dma((N_SUB,)),
            dma((N_SUB, n_half)),
            dma((N_SUB, n_half)),
            dma((N_SUB, blocks)),
            dma((blocks,)),
            dma((blocks, n_section)),
            dma((blocks, n_section)),
            dma((n_section, blocks)),
            dma((n_section, blocks)),
            dma, dma, dma, dma,
        ],
        compiler_params=pltpu.CompilerParams(
            collective_id=0, has_side_effects=True, vmem_limit_bytes=60 * 1024 * 1024
        ),
    )(scale, bias, pair.reshape(1, rows), inputs, up_w, down_w)


def solution(mesh):
    return jax.shard_map(
        local,
        mesh=mesh,
        in_specs=(
            P("section", "dp", None),
            P("section", None, "tensor"),
            P("section", "tensor", None),
            P("dp"),
            P(),
            P(),
        ),
        out_specs=(P(), P(("dp", "section", "tensor"), None), P(("dp", "section", "tensor"), None)),
        check_vma=False,
    )
```

time: 58.8 us -> 46.2 us (0.79)
  Pallas kernels: 52.4 us -> 38.6 us
  local copies, waits for them, and re-layouts: 0 us -> 3.23 us
  other arithmetic: 1.8 us -> 0 us
    pallas_call x1, Pallas kernels: 52.4 us -> 38.6 us  [local(): pl.pallas_call(functools.partial(kernel, dims), out_shape=(jax.ShapeDtype...]
    unnamed x0 -> x2, local copies, waits for them, and re-layouts: none -> 3.23 us
    select_n x1 -> x0, other arithmetic: 1.8 us -> none  [local(): jnp.where(first_core, theirs, mine)]
where the time goes in v1:
time: 46.2 us; the launch traced here: 45.5 us
  Pallas kernels  38.6 us (84%)
  between operations  3.68 us (8%)
  local copies, waits for them, and re-layouts  3.23 us (7%)
    pallas_call x1, Pallas kernels, local(): pl.pallas_call(functools.partial(kernel, dims), out_shape=(jax.ShapeDtype...  38.6 us
    unnamed x2, local copies, waits for them, and re-layouts  3.23 us

profile of v1, /device:TPU:1, one launch (start us, length us, event | category | flops | bytes accessed | tf_op | source)
XLA Modules:
  0.0 45.5 jit_solution(10079010202102333124)
XLA Ops:
  1.9 38.6 %shard_map.85 = (f32[1]{0:T(128)}, f32[48,1024]{1,0:T(8,128)}, f32[48,1024]{1,0:T(8,128)}) custom-call(f32[1]{0:T(128)S(6)} %copy.12.scale_ref, f32[1]{0:T(128)S(6)} %copy.13.bias_ref, s32[1,192]{1,0:T(1,128)} %bitcast.7, bf16[192,1024]{1,0:T(8,128)(2,1)} %bitcast.6, bf16[1024,2048]{1,0:T(8,128)(2,1)} %bitcast.4, bf16[2048,1024]{1,0:T(8,128)(2,1)} %bitcast.5), custom_call_target="tpu_custom_call" | custom-call | tf_op jit(solution)/shard_map/pallas_call | solution.py:501
  41.1 1.6 %copy.15 = f32[48,1024]{1,0:T(8,128)} copy(f32[48,1024]{1,0:T(8,128)} %get-tuple-element.7) | data formatting | bytes 393216
  42.7 1.6 %copy.16 = f32[48,1024]{1,0:T(8,128)} copy(f32[48,1024]{1,0:T(8,128)} %get-tuple-element.8) | data formatting | bytes 393216

commit v2 on v1

--- a/solution.py
+++ b/solution.py
@@ -16,10 +16,18 @@
 TOP = 32767.0
 
 
-def events():
-    hop = {"P": 0.0, "A": 2.3, "B": 2.9, "D": 5.2}
-    found = [(c * 0.8 + at, "PABD".index(kind), kind, c) for kind, at in hop.items() for c in range(N_SUB)]
-    return [(kind, c) for _, _, kind, c in sorted(found)]
+TIMES = (
+    {"A": (4.0, 0.40), "B": (3.9, 0.65), "D": (6.0, 0.65)},
+    {"A": (4.0, 0.50), "B": (4.1, 0.55), "D": (5.5, 0.65)},
+)
+
+
+def events(tower):
+    found = [
+        (start + c * step, "ABD".index(kind), kind, c)
+        for kind, (start, step) in TIMES[tower].items() for c in range(N_SUB)
+    ]
+    return [("P", c) for c in range(N_SUB)] + [(kind, c) for _, _, kind, c in sorted(found)]
 
 
 def wait_bytes(ref, sem):
@@ -58,24 +66,26 @@
 def kernel(
     dims,
     scale_ref, bias_ref, pair_ref, x_ref, up_ref, down_ref,
-    loss_out, slide_out, report_out,
+    loss_out, mine_out, theirs_out,
     xs, up, down, hid, part, fixed, fixed_in, unit, unit_in, units, pairs, left, right,
-    held, other, scores, grad, sent, sent_unit, got, got_unit, twin, loss_acc, loss_row, loss_all,
+    held, other, scores, grad, sent, sent_unit, relay, relay_unit, got, got_unit, twin,
+    loss_acc, loss_row, loss_all,
     x_sem, up_sem, down_sem, part_send, part_recv, unit_send, unit_recv, pair_send, pair_recv,
     held_recv, near_send, far_send, fwd_send, core_send, other_recv,
-    sent_send, sent_unit_send, got_recv, got_unit_recv, twin_send, twin_recv, loss_send, loss_recv,
+    sent_send, sent_unit_send, relay_recv, relay_unit_recv, got_recv, got_unit_recv,
+    twin_send, twin_recv, loss_send, loss_recv,
 ):
-    n_dp, n_section, n_tensor, n_half, total = dims
+    n_dp, n_section, n_tensor, n_near, total = dims
     quarter = xs.shape[0] // (n_section * n_tensor)
     own_rows = n_section * quarter
     rows_dp = xs.shape[0]
     d, s, x = lax.axis_index("dp"), lax.axis_index("section"), lax.axis_index("tensor")
-    y, low, half = lax.rem(d, INNER), lax.rem(d // INNER, PAIR), d // (INNER * PAIR)
+    y, near, far = lax.rem(d, INNER), lax.rem(d // INNER, n_near), d // (INNER * n_near)
     n_all = n_dp * n_section * n_tensor
     me = (d * n_section + s) * n_tensor + x
     tile_blocks = 2 * PAIR
     tile_rows = tile_blocks * own_rows
-    n_tiles = n_half // PAIR
+    n_tiles = n_near // PAIR
 
     def device_of(n):
         return {
@@ -88,20 +98,21 @@
         return first + t * (second - first)
 
     def member(t, a, b, core):
-        at_y, at_low, at_half = pick(t, y, a), pick(t, b, low), pick(t, half, b)
+        at_y, at_near, at_far = pick(t, y, a), pick(t, near, b), pick(t, b, far)
         return {
-            "dp": (at_half * PAIR + at_low) * INNER + at_y, "section": core, "tensor": pick(t, a, x)
+            "dp": (at_far * n_near + at_near) * INNER + at_y, "section": core,
+            "tensor": pick(t, a, x),
         }
 
     def place_of(t):
-        return pick(t, x, y), pick(t, low, half), pick(t, PAIR, n_half)
+        return pick(t, x, y), pick(t, far, near), pick(t, PAIR, n_near)
 
     my_a, my_b, my_n = place_of(s)
     mine = my_b * 2 + my_a
     partner = {"dp": d, "section": 1 - s, "tensor": x}
 
     def others(count, act):
-        if n_half == PAIR:
+        if n_near == PAIR:
             act(1)
         else:
             def body(k, carry):
@@ -155,14 +166,14 @@
         lane = iota((rows_dp, rows_dp), 1)
         t = step_of(lane, own_rows, n_tensor)
         hit = iota((rows_dp, rows_dp), 0) == natural(lane - t * own_rows, t)
-        pairs[low] = jnp.sum(jnp.where(hit, column, 0.0), axis=0, keepdims=True).astype(jnp.int32)
+        pairs[far] = jnp.sum(jnp.where(hit, column, 0.0), axis=0, keepdims=True).astype(jnp.int32)
 
     order_pairs()
 
     def report_ids(index):
         block = step_of(index, own_rows, tile_blocks)
         b = step_of(block, 2, PAIR)
-        home = (b * PAIR + low) * INNER + (block - 2 * b)
+        home = (far * n_near + b) * INNER + (block - 2 * b)
         return home * rows_dp + natural(index - block * own_rows, x)
 
     for c in x_copies:
@@ -218,29 +229,19 @@
     for c in range(N_SUB):
         part_copy(c).start()
     pair_copy = pltpu.make_async_remote_copy(
-        pairs.at[low], pairs.at[low], pair_send, pair_recv,
-        device_id={"dp": (half * PAIR + 1 - low) * INNER + y, "section": s, "tensor": x},
+        pairs.at[far], pairs.at[far], pair_send, pair_recv,
+        device_id={"dp": ((1 - far) * n_near + near) * INNER + y, "section": s, "tensor": x},
         device_id_type=MESH,
     )
     pair_copy.start()
 
     first(1)
     second(1)
+    right[...] = report_ids(iota((1, tile_rows), 1))
     pair_copy.wait_recv()
-
-    @pl.when(s == 0)
-    def _():
-        for b in range(PAIR):
-            column = to_column(pairs[b].astype(jnp.float32), rows_dp).astype(jnp.int32)
-            left[b * rows_dp:(b + 1) * rows_dp] = jnp.broadcast_to(column, (rows_dp, 128))
-        right[...] = report_ids(iota((1, tile_rows), 1))
-
-    @pl.when(s != 0)
-    def _():
-        left[...] = report_ids(iota((tile_rows, 128), 0))
-        for b in range(PAIR):
-            right[:, b * rows_dp:(b + 1) * rows_dp] = pairs[b]
-
+    for b in range(PAIR):
+        column = to_column(pairs[b].astype(jnp.float32), rows_dp).astype(jnp.int32)
+        left[b * rows_dp:(b + 1) * rows_dp] = jnp.broadcast_to(column, (rows_dp, 128))
     unit_copy.wait_recv()
     units[...] = jnp.broadcast_to(to_column(unit_in[...], own_rows), (own_rows, 128))
 
@@ -286,83 +287,25 @@
                 ].astype(jnp.float32)
                 norms = lax.rsqrt(jnp.sum(raw * raw, axis=-1, keepdims=True) + 1e-06)
                 held[mine, rows] = (raw * norms).astype(jnp.bfloat16)
+            others(my_n, lambda k: run(held_copy(mine, c, beyond(k), far_send.at[c, k])))
             run(held_copy(mine, c, beside, near_send.at[c]))
-            others(my_n, lambda k: run(held_copy(mine, c, beyond(k), far_send.at[c, k])))
             run(core_copy(mine, c))
         elif kind == "A":
-            block = my_b * 2 + 1 - my_a
-            arrived(block, c, begin)
-
-            @pl.when(s == 0)
-            def _():
-                others(my_n, lambda k: run(held_copy(block, c, beyond(k), fwd_send.at[c, k])))
+            arrived(my_b * 2 + 1 - my_a, c, begin)
         elif kind == "B":
             def from_b(k):
                 block = at_b(k) * 2 + my_a
-                arrived(block, c, begin)
-
-                @pl.when(s != 0)
-                def _():
-                    run(held_copy(block, c, beside, fwd_send.at[c, k]))
+                if begin:
+                    wait_bytes(piece(block, c), held_recv.at[c, block])
+                run(held_copy(block, c, beside, fwd_send.at[c, k]))
+                run(core_copy(block, c))
 
             others(my_n, from_b)
         else:
             others(my_n, lambda k: arrived(at_b(k) * 2 + 1 - my_a, c, begin))
 
-    for kind, c in events():
-        act_on(kind, c, True)
-
-    def other_block(block, carry):
-        wait_bytes(other.at[block], other_recv.at[block])
-        return carry
-
-    if n_half == PAIR:
-        for block in range(tile_blocks):
-            other_block(block, 0)
-    else:
-        lax.fori_loop(0, 2 * pick(s, n_half, PAIR), other_block, 0)
-
     scale_value, bias_value = scale_ref[0], bias_ref[0]
     width = held.shape[2]
-
-    def score(tile):
-        m_tile, t_tile = pick(s, 0, tile), pick(s, tile, 0)
-        rows = held[pl.ds(m_tile * tile_blocks, tile_blocks)].reshape(tile_rows, width)
-        columns = other[pl.ds(t_tile * tile_blocks, tile_blocks)].reshape(tile_rows, width)
-        logits = scale_value * lax.dot_general(
-            rows, columns, (((1,), (1,)), ((), ())), preferred_element_type=jnp.float32
-        ) + bias_value
-        shift = (1 - 2 * s) * tile * (PAIR * PAIR * INNER * rows_dp)
-        for j in range(tile_rows // 128):
-            lanes = slice(j * 128, (j + 1) * 128)
-            sign = jnp.where(left[...] == right[:, lanes] + shift, 1.0, -1.0).astype(jnp.float32)
-            u = -sign * logits[:, lanes]
-            e = jnp.exp(-jnp.abs(u))
-            loss_acc[...] += jnp.maximum(u, 0.0) + jnp.log1p(e)
-            sigmoid = jnp.where(u >= 0, 1.0, e) / (1.0 + e)
-            scores[:, lanes] = (-scale_value * sign * sigmoid).astype(jnp.bfloat16)
-        return m_tile, columns
-
-    if n_tiles > 1:
-        def clear(block, carry):
-            grad[block] = jnp.zeros_like(grad[block])
-            return carry
-
-        lax.fori_loop(0, 2 * my_n, clear, 0)
-
-        def tile_step(tile, carry):
-            m_tile, columns = score(tile)
-            for k in range(tile_blocks):
-                grad[m_tile * tile_blocks + k] += jnp.dot(
-                    scores[k * own_rows:(k + 1) * own_rows], columns,
-                    preferred_element_type=jnp.float32,
-                )
-            return carry
-
-        lax.fori_loop(0, n_tiles, tile_step, 0)
-    else:
-        _, columns = score(0)
-
     slot = d * n_tensor + x
 
     def loss_copy(n):
@@ -371,96 +314,214 @@
             device_id=device_of(n), device_id_type=MESH,
         )
 
-    def send_loss(n, carry):
-        loss_copy(lax.rem(me + n, n_all)).start()
-        return carry
-
-    def sent_copy(block, a, b, h):
+    def send_loss():
+        loss_row[...] = jnp.sum(loss_acc[...], axis=0, keepdims=True)
+        loss_all[slot] = loss_row[...]
+
+        def body(n, carry):
+            loss_copy(lax.rem(me + n, n_all)).start()
+            return carry
+
+        lax.fori_loop(1, n_all, body, 0)
+
+    def tile_of(ref, tile):
+        return ref[pl.ds(tile * tile_blocks, tile_blocks)].reshape(tile_rows, width)
+
+    def score(tower, block, tile):
+        slides, reports = (held, other) if tower == 0 else (other, held)
+        logits = scale_value * lax.dot_general(
+            slides[block], tile_of(reports, tile), (((1,), (1,)), ((), ())),
+            preferred_element_type=jnp.float32,
+        ) + bias_value
+        rows = pl.ds(pl.multiple_of(block * own_rows, 16), own_rows)
+        shift = tile * (PAIR * INNER * rows_dp)
+        for j in range(tile_rows // 128):
+            lanes = slice(j * 128, (j + 1) * 128)
+            sign = jnp.where(left[rows] == right[:, lanes] + shift, 1.0, -1.0).astype(jnp.float32)
+            u = -sign * logits[:, lanes]
+            e = jnp.exp(-jnp.abs(u))
+            if tower == 0:
+                loss_acc[...] += jnp.maximum(u, 0.0) + jnp.log1p(e)
+            sigmoid = jnp.where(u >= 0, 1.0, e) / (1.0 + e)
+            scores[rows, lanes] = (-scale_value * sign * sigmoid).astype(jnp.bfloat16)
+
+    def slide_terms(block, tile):
+        return jnp.dot(
+            scores[pl.ds(pl.multiple_of(block * own_rows, 16), own_rows)], tile_of(other, tile),
+            preferred_element_type=jnp.float32,
+        )
+
+    def report_terms():
+        return lax.dot_general(
+            scores[...], tile_of(other, 0), (((0,), (0,)), ((), ())),
+            preferred_element_type=jnp.float32,
+        ).reshape(tile_blocks, own_rows, width)
+
+    def sent_copy(block, c, target, to, sem):
         return pltpu.make_async_remote_copy(
-            sent.at[block, pl.ds(h * quarter, quarter)], got.at[s, mine], sent_send.at[block, h],
-            got_recv.at[s, mine], device_id=member(s, a, b, h), device_id_type=MESH,
-        )
-
-    def sent_unit_copy(block, a, b, h):
+            sent.at[block, pl.ds(c * sub, sub)], target, sent_send.at[block, c], sem,
+            device_id=to, device_id_type=MESH,
+        )
+
+    def sent_unit_copy(block, h, target, to, sem):
         return pltpu.make_async_remote_copy(
-            sent_unit.at[block, h], got_unit.at[s, mine], sent_unit_send.at[block, h],
-            got_unit_recv.at[s, mine], device_id=member(s, a, b, h), device_id_type=MESH,
-        )
-
-    def finish_block(block):
-        if n_tiles == 1:
-            grad[block] = jnp.dot(
-                scores[pl.ds(pl.multiple_of(block * own_rows, 16), own_rows)], columns,
-                preferred_element_type=jnp.float32,
-            )
-
-    def send_block(a, k, begin):
+            sent_unit.at[block, h], target, sent_unit_send.at[block, h], sem,
+            device_id=to, device_id_type=MESH,
+        )
+
+    def owner_unit_copy(block, h, a, b):
+        return sent_unit_copy(
+            block, h, got_unit.at[s, my_b], member(s, a, b, h), got_unit_recv.at[s, my_b]
+        )
+
+    def owner_copy(block, c, a, b):
+        per = N_SUB // n_section
+        return sent_copy(
+            block, c, got.at[s, my_b, pl.ds(c % per * sub, sub)], member(s, a, b, c // per),
+            got_recv.at[s, my_b],
+        )
+
+    def halves_to_rows(block, units_of):
+        for h in range(n_section):
+            sent_unit[block, h] = to_row(units_of[h * quarter:(h + 1) * quarter])
+
+    def send_across(k, begin):
         b = at_b(k)
-        block = b * 2 + a
+        block = b * 2 + 1 - my_a
+        copies = [sent_unit_copy(block, 0, relay_unit.at[b], beside, relay_unit_recv.at[b])]
+        copies += [
+            sent_copy(block, c, relay.at[b, pl.ds(c * sub, sub)], beside, relay_recv.at[b, c])
+            for c in range(N_SUB)
+        ]
         if begin:
-            finish_block(block)
             values, units_of = to_fixed(grad[block])
             sent[block] = values
-            for h in range(n_section):
-                sent_unit[block, h] = to_row(units_of[h * quarter:(h + 1) * quarter])
+            sent_unit[block, 0] = to_row(units_of)
+        for copy in copies:
+            copy.start() if begin else copy.wait_send()
+
+    def send_beside(begin):
+        block = my_b * 2 + 1 - my_a
+        if begin:
+            values, units_of = to_fixed(grad[block])
+            sent[block] = values
+            halves_to_rows(block, units_of)
         for h in range(n_section):
-            for copy in (sent_unit_copy(block, a, b, h), sent_copy(block, a, b, h)):
-                copy.start() if begin else copy.wait_send()
-
-    def send_all(begin):
-        others(my_n, lambda k: send_block(1 - my_a, k, begin))
-        others(my_n, lambda k: send_block(my_a, k, begin))
-        send_block(1 - my_a, 0, begin)
-
-    send_all(True)
-    finish_block(mine)
+            copy = owner_unit_copy(block, h, 1 - my_a, my_b)
+            copy.start() if begin else copy.wait_send()
+        for c in range(N_SUB):
+            copy = owner_copy(block, c, 1 - my_a, my_b)
+            copy.start() if begin else copy.wait_send()
+
+    def pass_on(k, begin):
+        b = at_b(k)
+        block = b * 2 + my_a
+        if begin:
+            top = jnp.max(jnp.abs(grad[block]), axis=-1, keepdims=True)
+            wait_bytes(relay_unit.at[b], relay_unit_recv.at[b])
+            came = to_column(relay_unit[b], own_rows)
+            units_of = jnp.maximum(top, 1e-30) * (1.0 / TOP) + came
+            halves_to_rows(block, units_of)
+            inverse = 1.0 / units_of
+        for h in range(n_section):
+            copy = owner_unit_copy(block, h, my_a, b)
+            copy.start() if begin else copy.wait_send()
+        for c in range(N_SUB):
+            if begin:
+                rows = slice(c * sub, (c + 1) * sub)
+                wait_bytes(relay.at[b, pl.ds(c * sub, sub)], relay_recv.at[b, c])
+                value = grad[block, rows] + from_fixed(relay[b, rows], came[rows])
+                sent[block, rows] = jnp.round(value * inverse[rows]).astype(jnp.int32).astype(jnp.int16)
+            copy = owner_copy(block, c, my_a, b)
+            copy.start() if begin else copy.wait_send()
+
     twin_copy = pltpu.make_async_remote_copy(
         grad.at[mine, pl.ds(pl.multiple_of((1 - s) * quarter, 16), quarter)], twin,
         twin_send, twin_recv, device_id=partner, device_id_type=MESH,
     )
-    twin_copy.start()
-    loss_row[...] = jnp.sum(loss_acc[...], axis=0, keepdims=True)
-
-    @pl.when(s == 0)
-    def _():
-        loss_all[slot] = loss_row[...]
-        lax.fori_loop(1, n_all, send_loss, 0)
-
-    def add_got(t, a, b, out):
-        block = b * 2 + a
-        wait_bytes(got_unit.at[t, block], got_unit_recv.at[t, block])
-        wait_bytes(got.at[t, block], got_recv.at[t, block])
-        out[...] += from_fixed(got[t, block], to_column(got_unit[t, block], quarter))
+
+    def other_block(block):
+        wait_bytes(other.at[block], other_recv.at[block])
+
+    def run_tower(tower):
+        for kind, c in events(tower):
+            act_on(kind, c, True)
+        if n_tiles > 1:
+            def wait_block(block, carry):
+                other_block(block)
+                return carry
+
+            lax.fori_loop(0, 2 * (n_near if tower == 0 else PAIR), wait_block, 0)
+            if tower == 0:
+                grad[0:tile_blocks] = jnp.zeros_like(grad[0:tile_blocks])
+
+            def tile_step(tile, carry):
+                for k in range(tile_blocks):
+                    score(tower, k, tile)
+                    if tower == 0:
+                        grad[k] += slide_terms(k, tile)
+                if tower == 1:
+                    grad[pl.ds(tile * tile_blocks, tile_blocks)] = report_terms()
+                return carry
+
+            lax.fori_loop(0, n_tiles, tile_step, 0)
+            others(my_n, lambda k: send_across(k, True))
+            send_beside(True)
+        elif tower == 0:
+            for block in range(tile_blocks):
+                other_block(block)
+            for block, send in (
+                ((1 - my_b) * 2 + 1 - my_a, lambda: send_across(1, True)),
+                (my_b * 2 + 1 - my_a, lambda: send_beside(True)),
+                ((1 - my_b) * 2 + my_a, lambda: None),
+                (mine, lambda: None),
+            ):
+                score(tower, block, 0)
+                grad[block] = slide_terms(block, 0)
+                send()
+        else:
+            for block in (
+                far * 2 + x, far * 2 + 1 - x, (1 - far) * 2 + x, (1 - far) * 2 + 1 - x,
+            ):
+                other_block(block)
+                score(tower, block, 0)
+            grad[...] = report_terms()
+            send_across(1, True)
+            send_beside(True)
+        if tower == 0:
+            send_loss()
+        twin_copy.start()
+        others(my_n, lambda k: pass_on(k, True))
+
+    for tower in range(n_section):
+        @pl.when(s == tower)
+        def _():
+            run_tower(tower)
+
+    def add_got(t, b, out):
+        wait_bytes(got_unit.at[t, b], got_unit_recv.at[t, b])
+        wait_bytes(got.at[t, b], got_recv.at[t, b])
+        out[...] += from_fixed(got[t, b], to_column(got_unit[t, b], quarter))
 
     def collect(t, out):
-        a, b, count = place_of(t)
-        add_got(t, 1 - a, b, out)
-        others(count, lambda k: add_got(t, a, lax.rem(b + k, count), out))
-        others(count, lambda k: add_got(t, 1 - a, lax.rem(b + k, count), out))
-
-    own_sum = grad[mine, pl.ds(pl.multiple_of(s * quarter, 16), quarter)]
+        _, b, count = place_of(t)
+        add_got(t, b, out)
+        others(count, lambda k: add_got(t, lax.rem(b + k, count), out))
+
+    mine_out[...] = grad[mine, pl.ds(pl.multiple_of(s * quarter, 16), quarter)]
     twin_copy.wait_recv()
-
-    @pl.when(s == 0)
-    def _():
-        slide_out[...] = own_sum
-        report_out[...] = twin[...]
-
-    @pl.when(s != 0)
-    def _():
-        report_out[...] = own_sum
-        slide_out[...] = twin[...]
-
-    collect(0, slide_out)
-    collect(1, report_out)
-
+    theirs_out[...] = twin[...]
+    collect(s, mine_out)
+    collect(1 - s, theirs_out)
     for c in range(N_SUB):
         part_copy(c).wait_send()
     unit_copy.wait_send()
     pair_copy.wait_send()
-    for kind, c in events():
+    for kind, c in events(0):
         act_on(kind, c, False)
-    send_all(False)
+    others(my_n, lambda k: send_across(k, False))
+    send_beside(False)
+    others(my_n, lambda k: pass_on(k, False))
     twin_copy.wait_send()
     n_chips = n_dp * n_tensor
 
@@ -487,8 +548,8 @@
     quarter = rows // group
     own_rows = n_section * quarter
     total = n_dp * rows
-    n_half = n_dp // (INNER * PAIR)
-    blocks = 2 * n_half
+    n_near = n_dp // (INNER * PAIR)
+    blocks = 2 * n_near
     tile_rows = 2 * PAIR * own_rows
 
     f32, bf16, i16, i32 = jnp.float32, jnp.bfloat16, jnp.int16, jnp.int32
@@ -497,8 +558,8 @@
     hbm = pl.BlockSpec(memory_space=pl.ANY)
     dma = pltpu.SemaphoreType.DMA
     n_all = n_dp * group
-    dims = (n_dp, n_section, n_tensor, n_half, total)
-    return pl.pallas_call(
+    dims = (n_dp, n_section, n_tensor, n_near, total)
+    loss, mine, theirs = pl.pallas_call(
         functools.partial(kernel, dims),
         out_shape=(
             jax.ShapeDtypeStruct((1,), f32),
@@ -527,10 +588,12 @@
             pltpu.VMEM((blocks, own_rows, width), f32),
             pltpu.VMEM((blocks, own_rows, width), i16),
             pltpu.VMEM((blocks, n_section, 1, 128), f32),
-            pltpu.VMEM((n_section, blocks, quarter, width), i16),
-            pltpu.VMEM((n_section, blocks, 1, 128), f32),
+            pltpu.VMEM((n_near, own_rows, width), i16),
+            pltpu.VMEM((n_near, 1, 128), f32),
+            pltpu.VMEM((n_section, n_near, quarter, width), i16),
+            pltpu.VMEM((n_section, n_near, 1, 128), f32),
             pltpu.VMEM((quarter, width), f32),
-            pltpu.VMEM((tile_rows, 128), f32),
+            pltpu.VMEM((own_rows, 128), f32),
             pltpu.VMEM((1, 128), f32),
             pltpu.VMEM((n_all, 1, 128), f32),
             dma((group,)),
@@ -541,20 +604,28 @@
             dma, dma, dma, dma,
             dma((N_SUB, blocks)),
             dma((N_SUB,)),
-            dma((N_SUB, n_half)),
-            dma((N_SUB, n_half)),
+            dma((N_SUB, n_near)),
+            dma((N_SUB, n_near)),
             dma((N_SUB, blocks)),
             dma((blocks,)),
+            dma((blocks, N_SUB)),
             dma((blocks, n_section)),
-            dma((blocks, n_section)),
-            dma((n_section, blocks)),
-            dma((n_section, blocks)),
+            dma((n_near, N_SUB)),
+            dma((n_near,)),
+            dma((n_section, n_near)),
+            dma((n_section, n_near)),
             dma, dma, dma, dma,
         ],
         compiler_params=pltpu.CompilerParams(
-            collective_id=0, has_side_effects=True, vmem_limit_bytes=60 * 1024 * 1024
+            collective_id=0, has_side_effects=True, vmem_limit_bytes=107 * 512 * 1024
         ),
     )(scale, bias, pair.reshape(1, rows), inputs, up_w, down_w)
+    first_core = lax.axis_index("section") == 0
+    return (
+        loss,
+        jnp.where(first_core, mine, theirs),
+        jnp.where(first_core, theirs, mine),
+    )
 
 
 def solution(mesh):

time: 46.2 us -> 40.5 us (0.88)
  Pallas kernels: 38.6 us -> 34.9 us
  local copies, waits for them, and re-layouts: 3.23 us -> 0.67 us
  other arithmetic: 0 us -> 0.78 us
    pallas_call x1, Pallas kernels: 38.6 us -> 34.9 us  [local(): pl.pallas_call(functools.partial(kernel, dims), out_shape=(jax.ShapeDtype...]
    unnamed x2, local copies, waits for them, and re-layouts: 3.23 us -> 0.67 us
    select_n x0 -> x1, other arithmetic: none -> 0.78 us  [local(): jnp.where(first_core, theirs, mine)]
where the time goes in v2:
time: 40.5 us; the launch traced here: 40 us
  Pallas kernels  34.9 us (86%)
  between operations  3.71 us (9%)
  other arithmetic  0.78 us (2%)
  local copies, waits for them, and re-layouts  0.67 us (2%)
    pallas_call x1, Pallas kernels, local(): pl.pallas_call(functools.partial(kernel, dims), out_shape=(jax.ShapeDtype...  34.9 us

profile of v2, /device:TPU:1, one launch (start us, length us, event | category | flops | bytes accessed | tf_op | source)
XLA Modules:
  0.0 40.0 jit_solution(1451337207536081667)
XLA Ops:
  1.9 0.0 copy-start
  1.9 0.7 %copy-done = s32[192]{0:T(256)S(1)} copy-done((s32[192]{0:T(256)S(1)}, s32[192]{0:T(256)}, u32[]{:S(2)}) %copy-start) | copy-done | bytes 792
  2.6 34.9 %shard_map.85 = (f32[1]{0:T(128)}, f32[48,1024]{1,0:T(8,128)S(1)}, f32[48,1024]{1,0:T(8,128)S(1)}) custom-call(f32[1]{0:T(128)S(6)} %copy.10.scale_ref, f32[1]{0:T(128)S(6)} %copy.11.bias_ref, s32[1,192]{1,0:T(1,128)S(1)} %bitcast.4, bf16[192,1024]{1,0:T(8,128)(2,1)} %bitcast.7, bf16[1024,2048]{1,0:T(8,128)(2,1)} %bitcast.5, bf16[2048,1024]{1,0:T(8,128)(2,1)} %bitcast.6), custom_call_target="tpu_custom_call" | custom-call | tf_op jit(solution)/shard_map/pallas_call | solution.py:562
  37.5 0.8 %broadcast_select_fusion = (f32[48,1024]{1,0:T(8,128)}, f32[48,1024]{1,0:T(8,128)}) fusion(f32[48,1024]{1,0:T(8,128)S(1)} %get-tuple-element.8, f32[48,1024]{1,0:T(8,128)S(1)} %get-tuple-element.7, pred[]{:T(512)S(6)} %eq.3), kind=kLoop, calls=%fused_computation | loop fusion | flops 98304 | bytes 786433 | tf_op jit(solution)/shard_map/jit(_where)/select_n | solution.py:627
Async XLA Ops:
  1.9 0.7 %copy-start = (s32[192]{0:T(256)S(1)}, s32[192]{0:T(256)}, u32[]{:S(2)}) copy-start(s32[192]{0:T(256)} %param.9) | copy-start | bytes 2308

commit v3 on v2

--- a/solution.py
+++ b/solution.py
@@ -17,8 +17,8 @@
 
 
 TIMES = (
-    {"A": (4.0, 0.40), "B": (3.9, 0.65), "D": (6.0, 0.65)},
-    {"A": (4.0, 0.50), "B": (4.1, 0.55), "D": (5.5, 0.65)},
+    {"A": (4.0, 0.40), "B": (3.2, 0.70), "D": (5.4, 0.70)},
+    {"A": (2.6, 0.50), "B": (2.7, 0.55), "D": (5.0, 0.55)},
 )
 
 
@@ -65,13 +65,13 @@
 
 def kernel(
     dims,
-    scale_ref, bias_ref, pair_ref, x_ref, up_ref, down_ref,
+    scale_in, bias_in, pair_in, x_ref, up_ref, down_ref,
     loss_out, mine_out, theirs_out,
     xs, up, down, hid, part, fixed, fixed_in, unit, unit_in, units, pairs, left, right,
     held, other, scores, grad, sent, sent_unit, relay, relay_unit, got, got_unit, twin,
-    loss_acc, loss_row, loss_all,
-    x_sem, up_sem, down_sem, part_send, part_recv, unit_send, unit_recv, pair_send, pair_recv,
-    held_recv, near_send, far_send, fwd_send, core_send, other_recv,
+    loss_acc, loss_row, loss_all, scale_ref, bias_ref, pair_ref,
+    small_sem, x_sem, up_sem, down_sem, part_send, part_recv, unit_send, unit_recv, pair_send, pair_recv,
+    held_recv, near_send, far_send, fwd_send, cross_send, core_send, other_recv,
     sent_send, sent_unit_send, relay_recv, relay_unit_recv, got_recv, got_unit_recv,
     twin_send, twin_recv, loss_send, loss_recv,
 ):
@@ -108,7 +108,10 @@
         return pick(t, x, y), pick(t, far, near), pick(t, PAIR, n_near)
 
     my_a, my_b, my_n = place_of(s)
-    mine = my_b * 2 + my_a
+    def block_of(a, b):
+        return (b // PAIR) * tile_blocks + a * PAIR + lax.rem(b, PAIR)
+
+    mine = block_of(my_a, my_b)
     partner = {"dp": d, "section": 1 - s, "tensor": x}
 
     def others(count, act):
@@ -128,17 +131,25 @@
                 xs.at[pl.ds(side * own_rows + q * quarter, quarter)],
                 x_sem.at[side * n_section + q],
             ))
+    small_copies = [
+        pltpu.make_async_copy(here, there, small_sem.at[i])
+        for i, (here, there) in enumerate(
+            ((pair_in, pair_ref), (scale_in, scale_ref), (bias_in, bias_ref))
+        )
+    ]
+    for c in small_copies:
+        c.start()
     for c in x_copies:
         c.start()
     up_w = up.shape[1] // UP_PARTS
     down_w = down.shape[1] // DOWN_PARTS
 
     def up_copy(i):
-        cols = pl.ds(pl.multiple_of(i * up_w, 128), up_w)
+        cols = pl.ds(i * up_w, up_w)
         return pltpu.make_async_copy(up_ref.at[:, cols], up.at[:, cols], up_sem.at[i])
 
     def down_copy(i):
-        cols = pl.ds(pl.multiple_of(i * down_w, 128), down_w)
+        cols = pl.ds(i * down_w, down_w)
         return pltpu.make_async_copy(down_ref.at[:, cols], down.at[:, cols], down_sem.at[i])
 
     for i in range(UP_PARTS):
@@ -168,12 +179,14 @@
         hit = iota((rows_dp, rows_dp), 0) == natural(lane - t * own_rows, t)
         pairs[far] = jnp.sum(jnp.where(hit, column, 0.0), axis=0, keepdims=True).astype(jnp.int32)
 
+    for c in small_copies:
+        c.wait()
     order_pairs()
 
     def report_ids(index):
         block = step_of(index, own_rows, tile_blocks)
-        b = step_of(block, 2, PAIR)
-        home = (far * n_near + b) * INNER + (block - 2 * b)
+        a = step_of(block, PAIR, 2)
+        home = (far * n_near + block - PAIR * a) * INNER + a
         return home * rows_dp + natural(index - block * own_rows, x)
 
     for c in x_copies:
@@ -185,25 +198,27 @@
         def body(i, carry):
             if side == 0:
                 up_copy(i).wait()
-            cols = pl.ds(pl.multiple_of(i * up_w, 128), up_w)
+            cols = pl.ds(i * up_w, up_w)
             h = jnp.dot(xs[rows], up[:, cols], preferred_element_type=jnp.float32)
             hid[rows, cols] = jax.nn.gelu(h).astype(jnp.bfloat16)
             return carry
 
-        lax.fori_loop(0, UP_PARTS, body, 0)
+        for i in range(UP_PARTS):
+            body(i, 0)
 
     def second(side):
         def body(i, carry):
             if side == 0:
                 down_copy(i).wait()
-            cols = pl.ds(pl.multiple_of(i * down_w, 128), down_w)
+            cols = pl.ds(i * down_w, down_w)
             part[:, cols] = jnp.dot(
                 hid[side * own_rows:(side + 1) * own_rows], down[:, cols],
                 preferred_element_type=jnp.float32,
             )
             return carry
 
-        lax.fori_loop(0, DOWN_PARTS, body, 0)
+        for i in range(DOWN_PARTS):
+            body(i, 0)
 
     first(0)
     second(0)
@@ -225,9 +240,16 @@
     unit_copy = pltpu.make_async_remote_copy(
         unit, unit_in, unit_send, unit_recv, device_id=across, device_id_type=MESH
     )
-    unit_copy.start()
-    for c in range(N_SUB):
-        part_copy(c).start()
+
+    def send_parts():
+        unit_copy.start()
+        for c in range(N_SUB):
+            part_copy(c).start()
+
+    @pl.when(s == 0)
+    def _():
+        send_parts()
+
     pair_copy = pltpu.make_async_remote_copy(
         pairs.at[far], pairs.at[far], pair_send, pair_recv,
         device_id={"dp": ((1 - far) * n_near + near) * INNER + y, "section": s, "tensor": x},
@@ -237,11 +259,11 @@
 
     first(1)
     second(1)
-    right[...] = report_ids(iota((1, tile_rows), 1))
-    pair_copy.wait_recv()
-    for b in range(PAIR):
-        column = to_column(pairs[b].astype(jnp.float32), rows_dp).astype(jnp.int32)
-        left[b * rows_dp:(b + 1) * rows_dp] = jnp.broadcast_to(column, (rows_dp, 128))
+
+    @pl.when(s == 1)
+    def _():
+        send_parts()
+
     unit_copy.wait_recv()
     units[...] = jnp.broadcast_to(to_column(unit_in[...], own_rows), (own_rows, 128))
 
@@ -261,6 +283,13 @@
         )
 
     beside = member(s, 1 - my_a, my_b, s)
+    beside_partner = member(s, 1 - my_a, my_b, 1 - s)
+
+    def cross_copy(block, c, sem):
+        return pltpu.make_async_remote_copy(
+            piece(block, c), other.at[block, pl.ds(c * sub, sub)], sem, other_recv.at[block],
+            device_id=beside_partner, device_id_type=MESH,
+        )
 
     def at_b(k):
         return lax.rem(my_b + k, my_n)
@@ -291,20 +320,25 @@
             run(held_copy(mine, c, beside, near_send.at[c]))
             run(core_copy(mine, c))
         elif kind == "A":
-            arrived(my_b * 2 + 1 - my_a, c, begin)
+            arrived(block_of(1 - my_a, my_b), c, begin)
         elif kind == "B":
             def from_b(k):
-                block = at_b(k) * 2 + my_a
+                block = block_of(my_a, at_b(k))
                 if begin:
                     wait_bytes(piece(block, c), held_recv.at[c, block])
+                run(cross_copy(block, c, cross_send.at[c, k]))
                 run(held_copy(block, c, beside, fwd_send.at[c, k]))
                 run(core_copy(block, c))
 
             others(my_n, from_b)
-        else:
-            others(my_n, lambda k: arrived(at_b(k) * 2 + 1 - my_a, c, begin))
-
-    scale_value, bias_value = scale_ref[0], bias_ref[0]
+        elif begin:
+            def from_both(k):
+                block = block_of(1 - my_a, at_b(k))
+                wait_bytes(piece(block, c), held_recv.at[c, block])
+
+            others(my_n, from_both)
+
+    scale_value, bias_value = scale_ref[...], bias_ref[...]
     width = held.shape[2]
     slot = d * n_tensor + x
 
@@ -327,29 +361,29 @@
     def tile_of(ref, tile):
         return ref[pl.ds(tile * tile_blocks, tile_blocks)].reshape(tile_rows, width)
 
-    def score(tower, block, tile):
+    def score(tower, a, tile):
         slides, reports = (held, other) if tower == 0 else (other, held)
         logits = scale_value * lax.dot_general(
-            slides[block], tile_of(reports, tile), (((1,), (1,)), ((), ())),
-            preferred_element_type=jnp.float32,
+            slides[pl.ds(a * PAIR, PAIR)].reshape(rows_dp, width), tile_of(reports, tile),
+            (((1,), (1,)), ((), ())), preferred_element_type=jnp.float32,
         ) + bias_value
-        rows = pl.ds(pl.multiple_of(block * own_rows, 16), own_rows)
+        rows = pl.ds(pl.multiple_of(a * rows_dp, 16), rows_dp)
         shift = tile * (PAIR * INNER * rows_dp)
         for j in range(tile_rows // 128):
             lanes = slice(j * 128, (j + 1) * 128)
             sign = jnp.where(left[rows] == right[:, lanes] + shift, 1.0, -1.0).astype(jnp.float32)
             u = -sign * logits[:, lanes]
             e = jnp.exp(-jnp.abs(u))
-            if tower == 0:
+            if tower == 1:
                 loss_acc[...] += jnp.maximum(u, 0.0) + jnp.log1p(e)
             sigmoid = jnp.where(u >= 0, 1.0, e) / (1.0 + e)
             scores[rows, lanes] = (-scale_value * sign * sigmoid).astype(jnp.bfloat16)
 
-    def slide_terms(block, tile):
+    def slide_terms(a, tile):
         return jnp.dot(
-            scores[pl.ds(pl.multiple_of(block * own_rows, 16), own_rows)], tile_of(other, tile),
+            scores[pl.ds(pl.multiple_of(a * rows_dp, 16), rows_dp)], tile_of(other, tile),
             preferred_element_type=jnp.float32,
-        )
+        ).reshape(PAIR, own_rows, width)
 
     def report_terms():
         return lax.dot_general(
@@ -387,7 +421,7 @@
 
     def send_across(k, begin):
         b = at_b(k)
-        block = b * 2 + 1 - my_a
+        block = block_of(1 - my_a, b)
         copies = [sent_unit_copy(block, 0, relay_unit.at[b], beside, relay_unit_recv.at[b])]
         copies += [
             sent_copy(block, c, relay.at[b, pl.ds(c * sub, sub)], beside, relay_recv.at[b, c])
@@ -401,7 +435,7 @@
             copy.start() if begin else copy.wait_send()
 
     def send_beside(begin):
-        block = my_b * 2 + 1 - my_a
+        block = block_of(1 - my_a, my_b)
         if begin:
             values, units_of = to_fixed(grad[block])
             sent[block] = values
@@ -415,7 +449,7 @@
 
     def pass_on(k, begin):
         b = at_b(k)
-        block = b * 2 + my_a
+        block = block_of(my_a, b)
         if begin:
             top = jnp.max(jnp.abs(grad[block]), axis=-1, keepdims=True)
             wait_bytes(relay_unit.at[b], relay_unit_recv.at[b])
@@ -443,9 +477,22 @@
     def other_block(block):
         wait_bytes(other.at[block], other_recv.at[block])
 
+    def make_ids():
+        right[...] = report_ids(iota((1, tile_rows), 1))
+        pair_copy.wait_recv()
+        for b in range(PAIR):
+            column = to_column(pairs[b].astype(jnp.float32), rows_dp).astype(jnp.int32)
+            for a in range(n_tensor):
+                at = (a * PAIR + b) * own_rows
+                left[at:at + own_rows] = jnp.broadcast_to(
+                    column[a * own_rows:(a + 1) * own_rows], (own_rows, 128)
+                )
+
     def run_tower(tower):
         for kind, c in events(tower):
             act_on(kind, c, True)
+            if (kind, c) == ("P", N_SUB - 1):
+                make_ids()
         if n_tiles > 1:
             def wait_block(block, carry):
                 other_block(block)
@@ -456,10 +503,10 @@
                 grad[0:tile_blocks] = jnp.zeros_like(grad[0:tile_blocks])
 
             def tile_step(tile, carry):
-                for k in range(tile_blocks):
-                    score(tower, k, tile)
+                for a in range(2):
+                    score(tower, a, tile)
                     if tower == 0:
-                        grad[k] += slide_terms(k, tile)
+                        grad[a * PAIR:(a + 1) * PAIR] += slide_terms(a, tile)
                 if tower == 1:
                     grad[pl.ds(tile * tile_blocks, tile_blocks)] = report_terms()
                 return carry
@@ -470,25 +517,21 @@
         elif tower == 0:
             for block in range(tile_blocks):
                 other_block(block)
-            for block, send in (
-                ((1 - my_b) * 2 + 1 - my_a, lambda: send_across(1, True)),
-                (my_b * 2 + 1 - my_a, lambda: send_beside(True)),
-                ((1 - my_b) * 2 + my_a, lambda: None),
-                (mine, lambda: None),
-            ):
-                score(tower, block, 0)
-                grad[block] = slide_terms(block, 0)
-                send()
+            score(tower, 1 - my_a, 0)
+            grad[pl.ds((1 - my_a) * PAIR, PAIR)] = slide_terms(1 - my_a, 0)
+            send_across(1, True)
+            send_beside(True)
+            score(tower, my_a, 0)
+            grad[pl.ds(my_a * PAIR, PAIR)] = slide_terms(my_a, 0)
         else:
-            for block in (
-                far * 2 + x, far * 2 + 1 - x, (1 - far) * 2 + x, (1 - far) * 2 + 1 - x,
-            ):
-                other_block(block)
-                score(tower, block, 0)
+            for a in (x, 1 - x):
+                for b in (far, 1 - far):
+                    other_block(block_of(a, b))
+                score(tower, a, 0)
             grad[...] = report_terms()
             send_across(1, True)
             send_beside(True)
-        if tower == 0:
+        if tower == 1:
             send_loss()
         twin_copy.start()
         others(my_n, lambda k: pass_on(k, True))
@@ -525,16 +568,16 @@
     twin_copy.wait_send()
     n_chips = n_dp * n_tensor
 
-    @pl.when(s == 0)
+    @pl.when(s == 1)
     def _():
         wait_bytes(loss_all.at[pl.ds(0, n_all - 1)], loss_send)
         wait_bytes(loss_all.at[pl.ds(0, n_chips - 1)], loss_recv)
 
-    @pl.when(s != 0)
+    @pl.when(s != 1)
     def _():
         wait_bytes(loss_all.at[pl.ds(0, n_chips)], loss_recv)
 
-    loss_out[0] = jnp.sum(loss_all[0:n_chips]) / total
+    loss_out[...] = jnp.broadcast_to(jnp.sum(loss_all[0:n_chips]) / total, loss_out.shape)
 
 
 def local(tower_input, up_weight, down_weight, pair, scale, bias):
@@ -554,7 +597,6 @@
 
     f32, bf16, i16, i32 = jnp.float32, jnp.bfloat16, jnp.int16, jnp.int32
     vmem = pl.BlockSpec(memory_space=pltpu.VMEM)
-    smem = pl.BlockSpec(memory_space=pltpu.SMEM)
     hbm = pl.BlockSpec(memory_space=pl.ANY)
     dma = pltpu.SemaphoreType.DMA
     n_all = n_dp * group
@@ -562,12 +604,12 @@
     loss, mine, theirs = pl.pallas_call(
         functools.partial(kernel, dims),
         out_shape=(
-            jax.ShapeDtypeStruct((1,), f32),
+            jax.ShapeDtypeStruct((1, 128), f32),
             jax.ShapeDtypeStruct((quarter, width), f32),
             jax.ShapeDtypeStruct((quarter, width), f32),
         ),
-        in_specs=[smem, smem, vmem, hbm, hbm, hbm],
-        out_specs=(smem, vmem, vmem),
+        in_specs=[hbm] * 6,
+        out_specs=(vmem, vmem, vmem),
         scratch_shapes=[
             pltpu.VMEM((rows, width), bf16),
             pltpu.VMEM((width, hidden), bf16),
@@ -593,9 +635,13 @@
             pltpu.VMEM((n_section, n_near, quarter, width), i16),
             pltpu.VMEM((n_section, n_near, 1, 128), f32),
             pltpu.VMEM((quarter, width), f32),
-            pltpu.VMEM((own_rows, 128), f32),
+            pltpu.VMEM((rows, 128), f32),
             pltpu.VMEM((1, 128), f32),
             pltpu.VMEM((n_all, 1, 128), f32),
+            pltpu.VMEM((1, 1), f32),
+            pltpu.VMEM((1, 1), f32),
+            pltpu.VMEM((1, rows), i32),
+            dma((3,)),
             dma((group,)),
             dma((UP_PARTS,)),
             dma((DOWN_PARTS,)),
@@ -604,6 +650,7 @@
             dma, dma, dma, dma,
             dma((N_SUB, blocks)),
             dma((N_SUB,)),
+            dma((N_SUB, n_near)),
             dma((N_SUB, n_near)),
             dma((N_SUB, n_near)),
             dma((N_SUB, blocks)),
@@ -617,12 +664,15 @@
             dma, dma, dma, dma,
         ],
         compiler_params=pltpu.CompilerParams(
-            collective_id=0, has_side_effects=True, vmem_limit_bytes=107 * 512 * 1024
+            collective_id=0, has_side_effects=True, vmem_limit_bytes=52 * 1024 * 1024
         ),
-    )(scale, bias, pair.reshape(1, rows), inputs, up_w, down_w)
+    )(scale.reshape(1, 1), bias.reshape(1, 1), *(
+        pltpu.with_memory_space_constraint(a, pltpu.HBM)
+        for a in (pair.reshape(1, rows), inputs, up_w, down_w)
+    ))
     first_core = lax.axis_index("section") == 0
     return (
-        loss,
+        loss[0, :1],
         jnp.where(first_core, mine, theirs),
         jnp.where(first_core, theirs, mine),
     )

time: 40.5 us -> 37.9 us (0.936)
  Pallas kernels: 34.9 us -> 33.8 us
  local copies, waits for them, and re-layouts: 0.67 us -> 0 us
  between operations: 3.71 us -> 3.1 us
    pallas_call x1, Pallas kernels: 34.9 us -> 33.8 us  [local(): pl.pallas_call(functools.partial(kernel, dims), out_shape=(jax.ShapeDtype...]
    unnamed x2 -> x0, local copies, waits for them, and re-layouts: 0.67 us -> none
where the time goes in v3:
time: 37.9 us; the launch traced here: 37.7 us
  Pallas kernels  33.8 us (89%)
  between operations  3.1 us (8%)
  other arithmetic  0.78 us (2%)
    pallas_call x1, Pallas kernels, local(): pl.pallas_call(functools.partial(kernel, dims), out_shape=(jax.ShapeDtype...  33.8 us
    select_n x1, other arithmetic, local(): jnp.where(first_core, theirs, mine)  0.78 us

profile of v3, /device:TPU:1, one launch (start us, length us, event | category | flops | bytes accessed | tf_op | source)
XLA Modules:
  0.0 37.7 jit_solution(16213931085898318170)
XLA Ops:
  1.9 33.8 %shard_map.85 = (f32[1,128]{1,0:T(1,128)S(1)}, f32[48,1024]{1,0:T(8,128)S(1)}, f32[48,1024]{1,0:T(8,128)S(1)}) custom-call(f32[1,1]{1,0:T(1,128)} %bitcast.8.scale_in, f32[1,1]{1,0:T(1,128)} %bitcast.9.bias_in, s32[1,192]{1,0:T(1,128)} %bitcast.14, bf16[192,1024]{1,0:T(8,128)(2,1)} %bitcast.13, bf16[1024,2048]{1,0:T(8,128)(2,1)} %bitcast.11, ...), custom_call_target="tpu_custom_call" | custom-call | tf_op jit(solution)/shard_map/pallas_call | solution.py:604
  35.7 0.8 %broadcast_select_fusion = (f32[48,1024]{1,0:T(8,128)}, f32[48,1024]{1,0:T(8,128)}) fusion(f32[48,1024]{1,0:T(8,128)S(1)} %get-tuple-element.8, f32[48,1024]{1,0:T(8,128)S(1)} %get-tuple-element.7, pred[]{:T(512)S(6)} %eq.3), kind=kLoop, calls=%fused_computation | loop fusion | flops 98304 | bytes 786433 | tf_op jit(solution)/shard_map/jit(_where)/select_n | solution.py:677

commit v4 on v3

--- a/solution.py
+++ b/solution.py
@@ -10,9 +10,10 @@
 MESH = pl.DeviceIdType.MESH
 INNER = 2
 PAIR = 2
-UP_PARTS = 4
-DOWN_PARTS = 2
+UP_PARTS = 2
+DOWN_PARTS = 1
 N_SUB = 6
+R_SUB = 6
 TOP = 32767.0
 
 
@@ -391,9 +392,11 @@
             preferred_element_type=jnp.float32,
         ).reshape(tile_blocks, own_rows, width)
 
+    part_rows = own_rows // R_SUB
+
     def sent_copy(block, c, target, to, sem):
         return pltpu.make_async_remote_copy(
-            sent.at[block, pl.ds(c * sub, sub)], target, sent_send.at[block, c], sem,
+            sent.at[block, pl.ds(c * part_rows, part_rows)], target, sent_send.at[block, c], sem,
             device_id=to, device_id_type=MESH,
         )
 
@@ -409,9 +412,9 @@
         )
 
     def owner_copy(block, c, a, b):
-        per = N_SUB // n_section
+        per = R_SUB // n_section
         return sent_copy(
-            block, c, got.at[s, my_b, pl.ds(c % per * sub, sub)], member(s, a, b, c // per),
+            block, c, got.at[s, my_b, pl.ds(c % per * part_rows, part_rows)], member(s, a, b, c // per),
             got_recv.at[s, my_b],
         )
 
@@ -424,8 +427,8 @@
         block = block_of(1 - my_a, b)
         copies = [sent_unit_copy(block, 0, relay_unit.at[b], beside, relay_unit_recv.at[b])]
         copies += [
-            sent_copy(block, c, relay.at[b, pl.ds(c * sub, sub)], beside, relay_recv.at[b, c])
-            for c in range(N_SUB)
+            sent_copy(block, c, relay.at[b, pl.ds(c * part_rows, part_rows)], beside, relay_recv.at[b, c])
+            for c in range(R_SUB)
         ]
         if begin:
             values, units_of = to_fixed(grad[block])
@@ -443,7 +446,7 @@
         for h in range(n_section):
             copy = owner_unit_copy(block, h, 1 - my_a, my_b)
             copy.start() if begin else copy.wait_send()
-        for c in range(N_SUB):
+        for c in range(R_SUB):
             copy = owner_copy(block, c, 1 - my_a, my_b)
             copy.start() if begin else copy.wait_send()
 
@@ -460,10 +463,10 @@
         for h in range(n_section):
             copy = owner_unit_copy(block, h, my_a, b)
             copy.start() if begin else copy.wait_send()
-        for c in range(N_SUB):
+        for c in range(R_SUB):
             if begin:
-                rows = slice(c * sub, (c + 1) * sub)
-                wait_bytes(relay.at[b, pl.ds(c * sub, sub)], relay_recv.at[b, c])
+                rows = slice(c * part_rows, (c + 1) * part_rows)
+                wait_bytes(relay.at[b, pl.ds(c * part_rows, part_rows)], relay_recv.at[b, c])
                 value = grad[block, rows] + from_fixed(relay[b, rows], came[rows])
                 sent[block, rows] = jnp.round(value * inverse[rows]).astype(jnp.int32).astype(jnp.int16)
             copy = owner_copy(block, c, my_a, b)
@@ -655,9 +658,9 @@
             dma((N_SUB, n_near)),
             dma((N_SUB, blocks)),
             dma((blocks,)),
-            dma((blocks, N_SUB)),
+            dma((blocks, R_SUB)),
             dma((blocks, n_section)),
-            dma((n_near, N_SUB)),
+            dma((n_near, R_SUB)),
             dma((n_near,)),
             dma((n_section, n_near)),
             dma((n_section, n_near)),

time: 37.9 us -> 37.3 us (0.984)
  Pallas kernels: 33.8 us -> 33.2 us
    pallas_call x1, Pallas kernels: 33.8 us -> 33.2 us  [local(): pl.pallas_call(functools.partial(kernel, dims), out_shape=(jax.ShapeDtype...]
where the time goes in v4:
time: 37.3 us; the launch traced here: 37.1 us
  Pallas kernels  33.2 us (89%)
  between operations  3.1 us (8%)
  other arithmetic  0.78 us (2%)
    pallas_call x1, Pallas kernels, local(): pl.pallas_call(functools.partial(kernel, dims), out_shape=(jax.ShapeDtype...  33.2 us
    select_n x1, other arithmetic, local(): jnp.where(first_core, theirs, mine)  0.78 us

profile of v4, /device:TPU:1, one launch (start us, length us, event | category | flops | bytes accessed | tf_op | source)
XLA Modules:
  0.0 37.1 jit_solution(1232136538925462460)
XLA Ops:
  1.9 33.2 %shard_map.85 = (f32[1,128]{1,0:T(1,128)S(1)}, f32[48,1024]{1,0:T(8,128)S(1)}, f32[48,1024]{1,0:T(8,128)S(1)}) custom-call(f32[1,1]{1,0:T(1,128)} %bitcast.8.scale_in, f32[1,1]{1,0:T(1,128)} %bitcast.9.bias_in, s32[1,192]{1,0:T(1,128)} %bitcast.14, bf16[192,1024]{1,0:T(8,128)(2,1)} %bitcast.13, bf16[1024,2048]{1,0:T(8,128)(2,1)} %bitcast.11, ...), custom_call_target="tpu_custom_call" | custom-call | tf_op jit(solution)/shard_map/pallas_call | solution.py:607
  35.2 0.8 %broadcast_select_fusion = (f32[48,1024]{1,0:T(8,128)}, f32[48,1024]{1,0:T(8,128)}) fusion(f32[48,1024]{1,0:T(8,128)S(1)} %get-tuple-element.8, f32[48,1024]{1,0:T(8,128)S(1)} %get-tuple-element.7, pred[]{:T(512)S(6)} %eq.3), kind=kLoop, calls=%fused_computation | loop fusion | flops 98304 | bytes 786433 | tf_op jit(solution)/shard_map/jit(_where)/select_n | solution.py:680

commit v5 on v4

--- a/solution.py
+++ b/solution.py
@@ -13,6 +13,7 @@
 UP_PARTS = 2
 DOWN_PARTS = 1
 N_SUB = 6
+DIRECT = 3
 R_SUB = 6
 TOP = 32767.0
 
@@ -327,15 +328,19 @@
                 block = block_of(my_a, at_b(k))
                 if begin:
                     wait_bytes(piece(block, c), held_recv.at[c, block])
-                run(cross_copy(block, c, cross_send.at[c, k]))
+                if c >= DIRECT:
+                    run(cross_copy(block, c, cross_send.at[c, k]))
                 run(held_copy(block, c, beside, fwd_send.at[c, k]))
                 run(core_copy(block, c))
 
             others(my_n, from_b)
-        elif begin:
+        else:
             def from_both(k):
                 block = block_of(1 - my_a, at_b(k))
-                wait_bytes(piece(block, c), held_recv.at[c, block])
+                if begin:
+                    wait_bytes(piece(block, c), held_recv.at[c, block])
+                if c < DIRECT:
+                    run(core_copy(block, c))
 
             others(my_n, from_both)
 

time: 37.3 us -> 36.9 us (0.989)
  no operation moved by 1% of the time
where the time goes in v5:
time: 36.9 us; the launch traced here: 36.8 us
  Pallas kernels  32.9 us (89%)
  between operations  3.1 us (8%)
  other arithmetic  0.78 us (2%)
    pallas_call x1, Pallas kernels, local(): pl.pallas_call(functools.partial(kernel, dims), out_shape=(jax.ShapeDtype...  32.9 us
    select_n x1, other arithmetic, local(): jnp.where(first_core, theirs, mine)  0.78 us

profile of v5, /device:TPU:1, one launch (start us, length us, event | category | flops | bytes accessed | tf_op | source)
XLA Modules:
  0.0 36.8 jit_solution(14906471604479802914)
XLA Ops:
  1.9 32.9 %shard_map.85 = (f32[1,128]{1,0:T(1,128)S(1)}, f32[48,1024]{1,0:T(8,128)S(1)}, f32[48,1024]{1,0:T(8,128)S(1)}) custom-call(f32[1,1]{1,0:T(1,128)} %bitcast.8.scale_in, f32[1,1]{1,0:T(1,128)} %bitcast.9.bias_in, s32[1,192]{1,0:T(1,128)} %bitcast.14, bf16[192,1024]{1,0:T(8,128)(2,1)} %bitcast.13, bf16[1024,2048]{1,0:T(8,128)(2,1)} %bitcast.11, ...), custom_call_target="tpu_custom_call" | custom-call | tf_op jit(solution)/shard_map/pallas_call | solution.py:612
  34.8 0.8 %broadcast_select_fusion = (f32[48,1024]{1,0:T(8,128)}, f32[48,1024]{1,0:T(8,128)}) fusion(f32[48,1024]{1,0:T(8,128)S(1)} %get-tuple-element.8, f32[48,1024]{1,0:T(8,128)S(1)} %get-tuple-element.7, pred[]{:T(512)S(6)} %eq.3), kind=kLoop, calls=%fused_computation | loop fusion | flops 98304 | bytes 786433 | tf_op jit(solution)/shard_map/jit(_where)/select_n | solution.py:685

commit v6 on v5

--- a/solution.py
+++ b/solution.py
@@ -13,7 +13,7 @@
 UP_PARTS = 2
 DOWN_PARTS = 1
 N_SUB = 6
-DIRECT = 3
+DIRECT = 2
 R_SUB = 6
 TOP = 32767.0
 
@@ -539,9 +539,9 @@
             grad[...] = report_terms()
             send_across(1, True)
             send_beside(True)
+        twin_copy.start()
         if tower == 1:
             send_loss()
-        twin_copy.start()
         others(my_n, lambda k: pass_on(k, True))
 
     for tower in range(n_section):

time: 36.9 us -> 37 us (level)
  no operation moved by 1% of the time
where the time goes in v6:
time: 37 us; the launch traced here: 36.8 us
  Pallas kernels  32.9 us (89%)
  between operations  3.1 us (8%)
  other arithmetic  0.78 us (2%)
    pallas_call x1, Pallas kernels, local(): pl.pallas_call(functools.partial(kernel, dims), out_shape=(jax.ShapeDtype...  32.9 us
    select_n x1, other arithmetic, local(): jnp.where(first_core, theirs, mine)  0.78 us

profile of v6, /device:TPU:1, one launch (start us, length us, event | category | flops | bytes accessed | tf_op | source)
XLA Modules:
  0.0 36.8 jit_solution(16627022952086449934)
XLA Ops:
  1.9 32.9 %shard_map.85 = (f32[1,128]{1,0:T(1,128)S(1)}, f32[48,1024]{1,0:T(8,128)S(1)}, f32[48,1024]{1,0:T(8,128)S(1)}) custom-call(f32[1,1]{1,0:T(1,128)} %bitcast.8.scale_in, f32[1,1]{1,0:T(1,128)} %bitcast.9.bias_in, s32[1,192]{1,0:T(1,128)} %bitcast.14, bf16[192,1024]{1,0:T(8,128)(2,1)} %bitcast.13, bf16[1024,2048]{1,0:T(8,128)(2,1)} %bitcast.11, ...), custom_call_target="tpu_custom_call" | custom-call | tf_op jit(solution)/shard_map/pallas_call | solution.py:612
  34.9 0.8 %broadcast_select_fusion = (f32[48,1024]{1,0:T(8,128)}, f32[48,1024]{1,0:T(8,128)}) fusion(f32[48,1024]{1,0:T(8,128)S(1)} %get-tuple-element.8, f32[48,1024]{1,0:T(8,128)S(1)} %get-tuple-element.7, pred[]{:T(512)S(6)} %eq.3), kind=kLoop, calls=%fused_computation | loop fusion | flops 98304 | bytes 786433 | tf_op jit(solution)/shard_map/jit(_where)/select_n | solution.py:685
